TPU v7x, 32 devices: a whole 2x2x4 slice. The times are simulated.
32 devices in a mesh: sky: 2 (over y), ma: 4 (over z), freq: 2 (over x), pol: 2 (over core).
Axes of the slice: x: 2, y: 2, z: 4, core: 2. Of those that a mesh axis runs over, the one named last changes fastest.
Arguments:
- alm: bfloat16 [2, 2, 1024, 4, 1024], P(None, 'freq', ('ma', 'pol'), None, 'sky'), parts along dimension 4, may hold values from -6 to 6
- beam: bfloat16 [4, 2, 2, 1024, 1024], P('ma', 'freq', None, 'pol'), may hold values from -0.1875 to 0.1875
- m_table: int32 [4], P('ma'), may hold values from 0 to 511, as said below
- chan_mask: int32 [2], P('freq'), may hold values from 0 to 1, as said below
- noise: float32 [2, 1024], P('freq', 'pol'), may hold values from 0.5 to 4
Outputs:
- scaled: bfloat16 [2, 2, 4, 1024, 1024], P(None, 'freq', 'ma', 'pol', 'sky'), parts along dimension 4
- channel_power: float32 [4], P(('sky', 'freq')), parts along dimension 0
There are 2 independent parts, one for each index of `sky`. A program takes and returns all parts, laid end to end along the dimension named above; an argument that names none is the same for every part. Nothing has to cross between parts.
Inputs may be any that keep to these rules, and one draw needn't show every extreme that they name: `m_table`: the 4 values are distinct whole numbers below 512. `chan_mask`: at least one of the 2 channels is usable.
All inputs are finite; a program needn't handle non-finite values.
Results may differ from a plain program's by a relative error of at most 0.00055.
Values may be sent and summed in bfloat16 or wider, within the bound.
A program may use at most 64 MiB of HBM per device.

v0:
```python
import functools

import jax
import jax.numpy as jnp
from jax import lax
from jax.experimental import pallas as pl
from jax.experimental.pallas import tpu as pltpu
from jax.sharding import PartitionSpec as P

MESH = pl.DeviceIdType.MESH


def arrival_order(n, i):
    return sorted((j for j in range(n) if j != i), key=lambda j: (abs(j - i), j))


def send_order(n, i):
    order = sorted((j for j in range(n) if j != i), key=lambda j: (abs(j - i), (j > i) != (2 * i < n)))
    return order[:1] + order[:0:-1] if i in (0, n - 1) else order


def others(n, me, rule):
    if n > 8:
        ups = [jnp.where(me + s < n, me + s, n - 1 - s) for s in range(1, n)]
        return ups
    table = [rule(n, i) for i in range(n)]
    order = []
    for k in range(n - 1):
        pick = jnp.int32(table[0][k])
        for i in range(1, n):
            pick = jnp.where(me == i, jnp.int32(table[i][k]), pick)
        order.append(pick)
    return order


def step_kernel(
    sizes, total, alm_ref, beam_ref, m_hbm, mask_hbm, noise_hbm, acc, scale_ref, power_ref,
    recv, wide, beam_v, inv_n, rs_n, mine, slots, m_ref, mask_ref, noise_ref,
    z_send, z_recv, p_send, p_recv, own_sem, beam_sem, q_send, q_recv, chain, meet, small_sem,
):
    n_ma, n_freq, n_pol = sizes
    n_all = n_ma * n_freq * n_pol
    ma, freq, pol = lax.axis_index("ma"), lax.axis_index("freq"), lax.axis_index("pol")
    block, columns = alm_ref.shape[2], alm_ref.shape[3]
    groups, _, rows, _ = recv.shape
    per_source = n_pol * block
    per_group = rows // per_source
    modes = beam_ref.shape[1]
    my_slot = (freq * n_ma + ma) * n_pol + pol

    def place(slot):
        return {"ma": lax.rem(slot // n_pol, n_ma), "freq": slot // (n_pol * n_ma), "pol": lax.rem(slot, n_pol)}

    def for_peers(body):
        if n_all <= 32:
            for r in range(1, n_all):
                body(r)
        else:
            lax.fori_loop(1, n_all, lambda r, _: (body(r), 0)[1], 0)

    beam_copy = pltpu.make_async_copy(beam_ref, beam_v, beam_sem)
    beam_copy.start()
    small = [
        pltpu.make_async_copy(src, dst, small_sem.at[i])
        for i, (src, dst) in enumerate(((m_hbm, m_ref), (mask_hbm, mask_ref), (noise_hbm, noise_ref)))
    ]
    for copy in small:
        copy.start()

    barrier = pltpu.get_barrier_semaphore()

    def tell_line(sem):
        @pl.when(ma > 0)
        def _():
            pl.semaphore_signal(sem, inc=1, device_id={"ma": ma - 1}, device_id_type=MESH)

        @pl.when(ma < n_ma - 1)
        def _():
            pl.semaphore_signal(sem, inc=1, device_id={"ma": ma + 1}, device_id_type=MESH)

    def tell(axis, me, n, sem):
        for q in range(1, n):
            pl.semaphore_signal(sem, inc=1, device_id={axis: lax.rem(me + q, n)}, device_id_type=MESH)

    beside = jnp.where(ma > 0, 1, 0) + jnp.where(ma < n_ma - 1, 1, 0)
    tell_line(barrier)
    tell("pol", pol, n_pol, barrier)
    tell("freq", freq, n_freq, barrier)

    def part(source, core, c):
        start = lax.rem(source, per_group) * per_source + core * block
        return recv.at[source // per_group, c, pl.ds(pl.multiple_of(start, block), block)]

    own = [pltpu.make_async_copy(alm_ref.at[ma, c], part(ma, pol, c), own_sem.at[c]) for c in range(2)]
    for copy in own:
        copy.start()
    pl.semaphore_wait(barrier, beside + n_pol - 1 + n_freq - 1)

    order = others(n_ma, ma, arrival_order)
    targets = others(n_ma, ma, send_order)
    sends = []

    def send(k):
        for c in range(2):
            sends.append(pltpu.make_async_remote_copy(
                src_ref=alm_ref.at[targets[k], c], dst_ref=part(ma, pol, c),
                send_sem=z_send.at[k, c], recv_sem=z_recv.at[ma, c],
                device_id={"ma": targets[k]}, device_id_type=MESH))
            sends[-1].start()

    if n_ma <= 8:
        send(0)
    for t in range(n_ma - 2):
        tell_line(chain.at[t])
        pl.semaphore_wait(chain.at[t], beside)
    for k in range(len(sends) // 2, n_ma - 1):
        send(k)

    def relay(source, c, src):
        hops = []
        for q in range(1, n_pol):
            hops.append(pltpu.make_async_remote_copy(
                src_ref=src, dst_ref=part(source, pol, c),
                send_sem=p_send.at[source, c], recv_sem=p_recv.at[source, c],
                device_id={"pol": lax.rem(pol + q, n_pol)}, device_id_type=MESH))
            hops[-1].start()
        return hops

    def arrival(source, c):
        return pltpu.make_async_remote_copy(
            src_ref=alm_ref.at[source, c], dst_ref=part(source, pol, c),
            send_sem=z_send.at[0, c], recv_sem=z_recv.at[source, c],
            device_id={"ma": source}, device_id_type=MESH)

    relays = [relay(ma, c, alm_ref.at[ma, c]) for c in range(2)]

    for copy in small:
        copy.wait()
    spread = jnp.transpose(jnp.broadcast_to(noise_ref[...], (128, modes)))
    inv_n[...] = 1.0 / spread
    rs_n[...] = lax.rsqrt(spread)
    mine[1:2, :] = jnp.full((1, 128), mask_ref[0].astype(jnp.float32))
    beam_copy.wait()
    strip = min(modes, 128)

    def widen(i, _):
        k0 = pl.multiple_of(i * strip, strip)
        for g in range(groups):
            degree = lax.broadcasted_iota(jnp.int32, (strip, rows), 1) + g * rows
            keep = degree >= m_ref[0]
            zero = jnp.zeros((strip, rows), jnp.float32)
            b0 = jnp.where(keep, beam_v[0, pl.ds(k0, strip), g * rows:(g + 1) * rows].astype(jnp.float32), zero)
            b1 = jnp.where(keep, beam_v[1, pl.ds(k0, strip), g * rows:(g + 1) * rows].astype(jnp.float32), zero)
            wide[g, 0, pl.ds(k0, strip), :] = b0.astype(wide.dtype)
            wide[g, 1, pl.ds(k0, strip), :] = (-b1).astype(wide.dtype)
            wide[g, 0, pl.ds(modes + k0, strip), :] = b1.astype(wide.dtype)
            wide[g, 1, pl.ds(modes + k0, strip), :] = b0.astype(wide.dtype)
        return 0

    lax.fori_loop(0, modes // strip, widen, 0)
    tell("pol", pol, n_pol, meet.at[0])
    pl.semaphore_wait(meet.at[0], n_pol - 1)
    tell("freq", freq, n_freq, meet.at[1])
    pl.semaphore_wait(meet.at[1], n_freq - 1)

    tile = min(modes, 512)
    tiles = 2 * modes // tile

    def accumulate(g, first):
        def body(i, _):
            k0 = pl.multiple_of(i * tile, tile)
            value = jnp.dot(wide[g, 0, pl.ds(k0, tile), :], recv[g, 0], preferred_element_type=jnp.float32)
            value += jnp.dot(wide[g, 1, pl.ds(k0, tile), :], recv[g, 1], preferred_element_type=jnp.float32)
            acc[pl.ds(k0, tile), :] = value if first else acc[pl.ds(k0, tile), :] + value
            return 0
        lax.fori_loop(0, tiles, body, 0)

    def squares(value, k0):
        noise_rows = inv_n[k0 % modes:k0 % modes + tile, :]
        sums = jnp.zeros((tile, 128), jnp.float32)
        for j in range(columns // 128):
            part_j = value[:, j * 128:(j + 1) * 128]
            sums += part_j * part_j
        return jnp.sum(sums * noise_rows, axis=0, keepdims=True)

    def finish(steps):
        power = jnp.zeros((1, 128), jnp.float32)
        for i in range(tiles):
            k0 = i * tile
            value = acc[k0:k0 + tile, :]
            for g, c in steps:
                value += jnp.dot(wide[g, c, k0:k0 + tile, :], recv[g, c], preferred_element_type=jnp.float32)
            acc[k0:k0 + tile, :] = value
            power += squares(value, k0)
        return power

    def add_half(g, c):
        for i in range(tiles):
            k0 = i * tile
            acc[k0:k0 + tile, :] += jnp.dot(wide[g, c, k0:k0 + tile, :], recv[g, c], preferred_element_type=jnp.float32)

    for copy in own:
        copy.wait()
    for c in range(2):
        for hop in relays[c]:
            hop.wait()
    if per_group == 1:
        accumulate(ma, True)
        for k, source in enumerate(order):
            later = []
            for c in range(2):
                arrival(source, c).wait_recv()
                later.append(relay(source, c, part(source, pol, c)))
            if k < len(order) - 1:
                for c in range(2):
                    for hop in later[c]:
                        hop.wait()
                accumulate(source, False)
            else:
                for hop in later[0]:
                    hop.wait()
                add_half(source, 0)
                for hop in later[1]:
                    hop.wait()
                power = finish([(source, 1)])
    else:
        later = []
        for source in order:
            for c in range(2):
                arrival(source, c).wait_recv()
                later.append(relay(source, c, part(source, pol, c)))
        for hops in later:
            for hop in hops:
                hop.wait()
        for g in range(groups):
            accumulate(g, g == 0)
        power = finish([])

    mine[0:1, :] = power
    slots[my_slot, 0:1, :] = power
    slots[my_slot, 1:2, :] = mine[1:2, :]

    def report(r):
        return pltpu.make_async_remote_copy(
            src_ref=mine, dst_ref=slots.at[my_slot], send_sem=q_send.at[r - 1], recv_sem=q_recv.at[my_slot],
            device_id=place(lax.rem(my_slot + r, n_all)), device_id_type=MESH)

    def heard(r):
        source = lax.rem(my_slot + r, n_all)
        pltpu.make_async_remote_copy(
            src_ref=mine, dst_ref=slots.at[source], send_sem=q_send.at[r - 1], recv_sem=q_recv.at[source],
            device_id=place(source), device_id_type=MESH).wait_recv()

    for_peers(lambda r: report(r).start())
    for copy in sends:
        copy.wait_send()
    for_peers(heard)

    per_freq = n_ma * n_pol
    masked, live, here = 0.0, 0.0, 0.0
    for f in range(n_freq):
        channel = jnp.sum(jnp.sum(slots[f * per_freq:(f + 1) * per_freq, 0, :], axis=0, keepdims=True), axis=1, keepdims=True) / total
        flag = slots[f * per_freq, 1:2, 0:1]
        masked += flag * channel
        live += flag
        here += jnp.where(freq == f, channel, 0.0)
    band = masked / live
    factor = mine[1:2, 0:1] / jnp.sqrt(0.5 * here + 0.5 * band + 1e-06)
    power_ref[...] = jnp.broadcast_to(here, power_ref.shape)
    scale_ref[...] = rs_n[...] * factor
    for_peers(lambda r: report(r).wait_send())


def rescale_kernel(acc, scale_ref, power_ref, out_ref, channel_ref, staged, sems):
    modes = scale_ref.shape[0]
    columns = acc.shape[1]
    strip = modes // sems.shape[0]
    channel_ref[0] = power_ref[0, 0]
    copies = []
    for i in range(sems.shape[0]):
        k0 = i * strip
        scale = scale_ref[k0:k0 + strip, :]
        for c in range(2):
            for j in range(columns // 128):
                value = acc[c * modes + k0:c * modes + k0 + strip, j * 128:(j + 1) * 128]
                staged[c, k0:k0 + strip, j * 128:(j + 1) * 128] = (value * scale).astype(staged.dtype)
        copies.append(pltpu.make_async_copy(
            staged.at[:, pl.ds(k0, strip)], out_ref.at[:, pl.ds(k0, strip)], sems.at[i]))
        copies[-1].start()
    for copy in copies:
        copy.wait()


def on_device(sizes, alm, beam, m_table, chan_mask, noise):
    n_ma, n_freq, n_pol = sizes
    planes = jnp.transpose(alm[:, 0], (2, 0, 1, 3))
    response = beam[0, 0]
    block, columns = planes.shape[2], planes.shape[3]
    modes, degrees = response.shape[1], response.shape[2]
    per_source = n_pol * block
    rows = per_source * max(1, min(n_ma, 256 // per_source))
    groups = degrees // rows
    n_all = n_ma * n_freq * n_pol
    total = float(n_ma * modes * n_pol * columns)
    vmem = pl.BlockSpec(memory_space=pltpu.VMEM)
    smem = pl.BlockSpec(memory_space=pltpu.SMEM)
    dma = pltpu.SemaphoreType.DMA
    hbm = pl.BlockSpec(memory_space=pl.ANY)
    visibility, scale, power = pl.pallas_call(
        functools.partial(step_kernel, sizes, total),
        out_shape=(
            jax.ShapeDtypeStruct((2 * modes, columns), jnp.float32),
            jax.ShapeDtypeStruct((modes, 128), jnp.float32),
            jax.ShapeDtypeStruct((1, 128), jnp.float32),
        ),
        in_specs=[vmem, hbm, hbm, hbm, hbm],
        out_specs=(vmem, vmem, vmem),
        scratch_shapes=[
            pltpu.VMEM((groups, 2, rows, columns), jnp.bfloat16),
            pltpu.VMEM((groups, 2, 2 * modes, rows), jnp.bfloat16),
            pltpu.VMEM((2, modes, degrees), jnp.bfloat16),
            pltpu.VMEM((modes, 128), jnp.float32),
            pltpu.VMEM((modes, 128), jnp.float32),
            pltpu.VMEM((2, 128), jnp.float32),
            pltpu.VMEM((n_all, 2, 128), jnp.float32),
            pltpu.SMEM((1,), jnp.int32),
            pltpu.SMEM((1,), jnp.int32),
            pltpu.VMEM((1, modes), jnp.float32),
            dma((n_ma, 2)), dma((n_ma, 2)), dma((n_ma, 2)), dma((n_ma, 2)), dma((2,)), dma,
            dma((n_all,)), dma((n_all,)),
            pltpu.SemaphoreType.REGULAR((max(1, n_ma - 2),)), pltpu.SemaphoreType.REGULAR((2,)), dma((3,)),
        ],
        compiler_params=pltpu.CompilerParams(collective_id=0, has_side_effects=True, vmem_limit_bytes=40 * 1024 * 1024),
        name="driftscan_step",
    )(planes, response, m_table, chan_mask, noise)
    pieces = 4 if modes % 64 == 0 else 1
    scaled, channel_power = pl.pallas_call(
        rescale_kernel,
        out_shape=(
            jax.ShapeDtypeStruct((2, modes, columns), jnp.bfloat16),
            jax.ShapeDtypeStruct((1,), jnp.float32),
        ),
        in_specs=[vmem, vmem, vmem],
        out_specs=(hbm, smem),
        scratch_shapes=[pltpu.VMEM((2, modes, columns), jnp.bfloat16), dma((pieces,))],
        compiler_params=pltpu.CompilerParams(vmem_limit_bytes=16 * 1024 * 1024),
        name="rescale",
    )(visibility, scale, power)
    return scaled[:, None, None], channel_power


def solution(mesh):
    sizes = (mesh.shape["ma"], mesh.shape["freq"], mesh.shape["pol"])
    return jax.shard_map(
        functools.partial(on_device, sizes),
        mesh=mesh,
        in_specs=(
            P(None, "freq", ("ma", "pol"), None, "sky"),
            P("ma", "freq", None, "pol", None),
            P("ma"),
            P("freq"),
            P("freq", "pol"),
        ),
        out_specs=(P(None, "freq", "ma", "pol", "sky"), P(("sky", "freq"))),
        check_vma=False,
    )
```

profile of v0, /device:TPU:0, one launch (start us, length us, event | category | flops | bytes accessed | tf_op | source)
XLA Modules:
  0.0 42.4 jit_solution(7920503400327475124)
XLA Ops:
  0.6 0.0 copy-start.1
  0.6 0.0 copy-start
  2.1 1.4 %copy.10 = bf16[2,1,128,4,512]{4,2,0,3,1:T(8,128)(2,1)S(1)} copy(bf16[2,1,128,4,512]{4,3,2,1,0:T(4,128)(2,1)} %param.5) | data formatting | bytes 2097152 | tf_op args[0]
  3.5 0.0 copy-done.1
  3.5 0.0 copy-done
  3.5 37.3 %driftscan_step.1 = (f32[1024,512]{1,0:T(8,128)S(1)}, f32[512,128]{1,0:T(8,128)S(1)}, f32[1,128]{1,0:T(1,128)S(1)}) custom-call(bf16[4,2,128,512]{3,2,1,0:T(8,128)(2,1)S(1)} %bitcast.9, bf16[2,512,1024]{2,1,0:T(8,128)(2,1)S(1)} %bitcast.10, s32[1]{0:T(128)S(6)} %copy.11.m_hbm, s32[1]{0:T(128)S(6)} %copy.12.mask_hbm, f32[1,512]{1,0:T(1,128)S(1)} %copy-done.1), custom_call_target="tpu_custom_call" | custom-call | tf_op jit(solution)/shard_map/driftscan_step/pallas_call | solution.py:309
  40.8 1.6 %rescale.1 = (bf16[2,512,512]{2,1,0:T(8,128)(2,1)}, f32[1]{0:T(128)}) custom-call(f32[1024,512]{1,0:T(8,128)S(1)} %get-tuple-element.7.acc, f32[512,128]{1,0:T(8,128)S(1)} %get-tuple-element.8.scale_ref, f32[1,128]{1,0:T(1,128)S(1)} %get-tuple-element.9.power_ref), custom_call_target="tpu_custom_call" | custom-call | tf_op jit(solution)/shard_map/rescale/pallas_call | solution.py:337
Async XLA Ops:
  0.6 2.9 %copy-start.1 = (f32[1,512]{1,0:T(1,128)S(1)}, f32[1,512]{1,0:T(1,128)}, u32[]{:S(2)}) copy-start(f32[1,512]{1,0:T(1,128)} %noise_hbm.1) | copy-start | bytes 6148
  0.6 2.9 %copy-start = (bf16[1,1,2,512,1024]{4,3,2,1,0:T(8,128)(2,1)S(1)}, bf16[1,1,2,512,1024]{4,3,2,1,0:T(8,128)(2,1)}, u32[]{:S(2)}) copy-start(bf16[1,1,2,512,1024]{4,3,2,1,0:T(8,128)(2,1)} %param.6) | copy-start | bytes 6291460
where the time goes:
time: 42.5 us; the launch traced here: 42.4 us
  Pallas kernels  38.8 us (91%)
  between operations  2.12 us (5%)
  local copies, waits for them, and re-layouts  1.43 us (3%)
    pallas_call x1, Pallas kernels, on_device(): pl.pallas_call(functools.partial(step_kernel, sizes, total), out_shape=(j...  37.3 us
    pallas_call x1, Pallas kernels, on_device(): pl.pallas_call(rescale_kernel, out_shape=(jax.ShapeDtypeStruct((2, modes,...  1.57 us
    unnamed x5, local copies, waits for them, and re-layouts  1.43 us

commit v1 on v0

v1 whole, which is shorter than its diff:
```python
import contextlib
import functools

import jax
import jax.numpy as jnp
from jax import lax
from jax.experimental import pallas as pl
from jax.experimental.pallas import tpu as pltpu
from jax.sharding import PartitionSpec as P

MESH = pl.DeviceIdType.MESH
LANES = 128


def mark(name):
    return contextlib.nullcontext()


def across(n, i):
    return n // 2 if 2 * i < n else n // 2 - 1


def processing_order(n, i):
    last = across(n, i)
    rest = sorted((j for j in range(n) if j not in (i, last)), key=lambda j: (-abs(j - i), j))
    return rest + ([last] if last != i else [])


def far_first(n, i):
    return sorted((j for j in range(n) if j != i), key=lambda j: (-abs(j - i), j))


def pick_by(me, values):
    pick = jnp.int32(values[0])
    for i in range(1, len(values)):
        pick = jnp.where(me == i, jnp.int32(values[i]), pick)
    return pick


def step_kernel(
    sizes, total, alm_hbm, beam_hbm, m_hbm, mask_hbm, noise_hbm, acc, scale_ref, power_ref,
    staged, planes, recv, wide, beam_v, inv_n, rs_n, mine, slots, m_ref, mask_ref, noise_ref,
    z_send, z_recv, p_send, p_recv, in_sem, beam_sem, q_send, q_recv, chain, meet, small_sem,
):
    n_ma, n_freq, n_pol = sizes
    n_all = n_ma * n_freq * n_pol
    ma, freq, pol = lax.axis_index("ma"), lax.axis_index("freq"), lax.axis_index("pol")
    block = staged.shape[1]
    groups, splits, _, rows, lanes = recv.shape
    per_source = n_pol * block
    per_group = rows // per_source
    modes = beam_hbm.shape[1]
    my_slot = (freq * n_ma + ma) * n_pol + pol
    few = n_ma <= 8 and per_group == 1

    def place(slot):
        return {"ma": lax.rem(slot // n_pol, n_ma), "freq": slot // (n_pol * n_ma), "pol": lax.rem(slot, n_pol)}

    def loop(low, high, body, unroll=False):
        if unroll:
            for r in range(low, high):
                body(r)
        else:
            lax.fori_loop(low, high, lambda r, _: (body(r), 0)[1], 0)

    def for_peers(body):
        loop(1, n_all, body, n_all <= 32)

    barrier = pltpu.get_barrier_semaphore()

    def tell_line(sem):
        @pl.when(ma > 0)
        def _():
            pl.semaphore_signal(sem, inc=1, device_id={"ma": ma - 1}, device_id_type=MESH)

        @pl.when(ma < n_ma - 1)
        def _():
            pl.semaphore_signal(sem, inc=1, device_id={"ma": ma + 1}, device_id_type=MESH)

    def tell(axis, me, n, sem):
        for q in range(1, n):
            pl.semaphore_signal(sem, inc=1, device_id={axis: lax.rem(me + q, n)}, device_id_type=MESH)

    beside = jnp.where(ma > 0, 1, 0) + jnp.where(ma < n_ma - 1, 1, 0)
    tell_line(barrier)
    tell("pol", pol, n_pol, barrier)
    tell("freq", freq, n_freq, barrier)

    pieces = in_sem.shape[1]
    size = block // pieces
    loads = [
        [pltpu.make_async_copy(
            alm_hbm.at[c, pl.ds(h * size, size)], staged.at[c, pl.ds(h * size, size)], in_sem.at[c, h])
         for h in range(pieces)] for c in range(2)
    ]
    for h in range(pieces):
        for c in range(2):
            loads[c][h].start()
    small = [
        pltpu.make_async_copy(src, dst, small_sem.at[i])
        for i, (src, dst) in enumerate(((m_hbm, m_ref), (mask_hbm, mask_ref), (noise_hbm, noise_ref)))
    ]
    for copy in small:
        copy.start()
    beam_copy = pltpu.make_async_copy(beam_hbm, beam_v, beam_sem)
    beam_copy.start()

    def part(source, core, j):
        start = lax.rem(source, per_group) * per_source + core * block
        return recv.at[source // per_group, j, :, pl.ds(pl.multiple_of(start, block), block)]

    step = min(size, 16)
    for h in range(pieces):
        for c in range(2):
            loads[c][h].wait()
            for e in range(h * size, (h + 1) * size, step):
                turned = jnp.transpose(staged[c, e:e + step], (1, 0, 2))
                for j in range(splits):
                    planes[:, j, c, e:e + step, :] = turned[:, :, j * lanes:(j + 1) * lanes]

    with mark("barrier"):
        pl.semaphore_wait(barrier, beside + n_pol - 1 + n_freq - 1)

    def send(target, j):
        return pltpu.make_async_remote_copy(
            src_ref=planes.at[target, j], dst_ref=part(ma, pol, j),
            send_sem=z_send.at[target, j], recv_sem=z_recv.at[ma, j],
            device_id={"ma": target}, device_id_type=MESH)

    def arrival(source, j):
        return pltpu.make_async_remote_copy(
            src_ref=planes.at[source, j], dst_ref=part(source, pol, j),
            send_sem=z_send.at[source, j], recv_sem=z_recv.at[source, j],
            device_id={"ma": source}, device_id_type=MESH)

    def hop(source, j, q, src):
        return pltpu.make_async_remote_copy(
            src_ref=src, dst_ref=part(source, pol, j),
            send_sem=p_send.at[source, j], recv_sem=p_recv.at[source, j],
            device_id={"pol": lax.rem(pol + q, n_pol)}, device_id_type=MESH)

    def relay(source, j, src=None):
        for q in range(1, n_pol):
            hop(source, j, q, part(source, pol, j) if src is None else src).start()

    def relayed(source, j):
        for q in range(1, n_pol):
            pltpu.make_async_remote_copy(
                src_ref=part(source, pol, j), dst_ref=part(source, lax.rem(pol + q, n_pol), j),
                send_sem=p_send.at[source, j], recv_sem=p_recv.at[source, j],
                device_id={"pol": lax.rem(pol + q, n_pol)}, device_id_type=MESH).wait_recv()

    early = {}
    if few:
        for i in range(n_ma):
            first = [(t, 0) for t in far_first(n_ma, i) if abs(t - i) == 1]
            later = [(t, j) for t in far_first(n_ma, i) for j in range(splits) if (t, j) not in first]
            early[i] = (first, later, max(i, n_ma - 1 - i) - 1)

    def send_phase(phase):
        for i in range(n_ma):
            first, later, when = early[i]
            now = (first if phase == 0 else []) + (later if phase == when else [])
            if now:
                @pl.when(ma == i)
                def _():
                    for t, j in now:
                        send(t, j).start()

    if few:
        send_phase(0)
    for t in range(n_ma - 2):
        tell_line(chain.at[t])
        pl.semaphore_wait(chain.at[t], beside)
        if few:
            send_phase(t + 1)
    if not few:
        for j in range(splits):
            loop(1, n_ma, lambda q: send(lax.rem(ma + q, n_ma), j).start())

    for j in range(splits):
        relay(ma, j, planes.at[ma, j])
        for c in range(2):
            part(ma, pol, j)[c] = planes[ma, j, c]

    for copy in small:
        copy.wait()
    spread = jnp.transpose(jnp.broadcast_to(noise_ref[...], (LANES, modes)))
    inv_n[...] = 1.0 / spread
    rs_n[...] = lax.rsqrt(spread)
    mine[1:2, :] = jnp.full((1, LANES), mask_ref[0, 0].astype(jnp.float32))
    beam_copy.wait()
    strip = min(modes, 128)

    def widen(i):
        k0 = pl.multiple_of(i * strip, strip)
        for g in range(groups):
            degree = lax.broadcasted_iota(jnp.int32, (strip, rows), 1) + g * rows
            keep = degree >= m_ref[0, 0]
            zero = jnp.zeros((strip, rows), jnp.float32)
            b0 = jnp.where(keep, beam_v[0, pl.ds(k0, strip), g * rows:(g + 1) * rows].astype(jnp.float32), zero)
            b1 = jnp.where(keep, beam_v[1, pl.ds(k0, strip), g * rows:(g + 1) * rows].astype(jnp.float32), zero)
            wide[g, pl.ds(k0, strip), 0:rows] = b0.astype(wide.dtype)
            wide[g, pl.ds(k0, strip), rows:2 * rows] = (-b1).astype(wide.dtype)
            wide[g, pl.ds(modes + k0, strip), 0:rows] = b1.astype(wide.dtype)
            wide[g, pl.ds(modes + k0, strip), rows:2 * rows] = b0.astype(wide.dtype)

    with mark("widen"):
        loop(0, modes // strip, widen)
    tell("pol", pol, n_pol, meet.at[0])
    pl.semaphore_wait(meet.at[0], n_pol - 1)
    tell("freq", freq, n_freq, meet.at[1])
    pl.semaphore_wait(meet.at[1], n_freq - 1)

    def product(g, j, k0, core=None):
        if core is None:
            return jnp.dot(wide[g, pl.ds(k0, modes), :], recv[g, j].reshape(2 * rows, lanes),
                           preferred_element_type=jnp.float32)
        start = pl.multiple_of(core * block, block)
        left = jnp.concatenate([wide[g, pl.ds(k0, modes), pl.ds(pl.multiple_of(c * rows + start, block), block)]
                                for c in range(2)], axis=1)
        right = jnp.concatenate([recv[g, j, c, pl.ds(start, block), :] for c in range(2)], axis=0)
        return jnp.dot(left, right, preferred_element_type=jnp.float32)

    def add(g, j, first=False, core=None):
        def body(i):
            k0 = pl.multiple_of(i * modes, modes)
            at = (pl.ds(k0, modes), slice(j * lanes, (j + 1) * lanes))
            value = product(g, j, k0, core)
            acc[at] = value if first else acc[at] + value
        loop(0, 2, body)

    def finish(g, j, power, core=None):
        def body(i, power):
            k0 = pl.multiple_of(i * modes, modes)
            at = (pl.ds(k0, modes), slice(j * lanes, (j + 1) * lanes))
            value = acc[at]
            if g is not None:
                value = value + product(g, j, k0, core)
                acc[at] = value
            weighted = value * value * inv_n[...]
            return power + jnp.sum(weighted.reshape(modes // 8, 8, lanes), axis=0)
        return lax.fori_loop(0, 2, body, power)

    power = jnp.zeros((8, lanes), jnp.float32)
    if few:
        split_last = n_pol == 2
        order = [pick_by(ma, [processing_order(n_ma, i)[k] for i in range(n_ma)]) for k in range(n_ma - 1)]
        with mark("own"):
            for j in range(splits):
                relayed(ma, j)
                add(ma, j, first=True)
        steps = [(k, j) for k in range(n_ma - 1) for j in range(splits)]

        def settle(k, j, power):
            with mark(f"relay{k}_{j}"):
                relayed(order[k], j)
            if k < n_ma - 2:
                add(order[k], j)
                return power
            return finish(order[k], j, power)

        for s, (k, j) in enumerate(steps):
            with mark(f"wait{k}_{j}"):
                arrival(order[k], j).wait_recv()
            relay(order[k], j)
            if s:
                power = settle(*steps[s - 1], power)
        k, j = steps[-1]
        if split_last:
            add(order[k], j, core=pol)
            with mark("relaylast"):
                relayed(order[k], j)
            power = finish(order[k], j, power, core=1 - pol)
        else:
            power = settle(k, j, power)
    else:
        for j in range(splits):
            def pass_on(q):
                source = lax.rem(ma + q, n_ma)
                arrival(source, j).wait_recv()
                relay(source, j)
            loop(1, n_ma, pass_on)
        for j in range(splits):
            loop(0, n_ma, lambda source: relayed(source, j))
            for g in range(groups):
                add(g, j, first=g == 0)
            power = finish(None, j, power)

    row = jnp.sum(power, axis=0, keepdims=True)
    mine[0:1, :] = row
    slots[my_slot, 0:1, :] = row
    slots[my_slot, 1:2, :] = mine[1:2, :]

    def report(r):
        return pltpu.make_async_remote_copy(
            src_ref=mine, dst_ref=slots.at[my_slot], send_sem=q_send.at[r - 1], recv_sem=q_recv.at[my_slot],
            device_id=place(lax.rem(my_slot + r, n_all)), device_id_type=MESH)

    def heard(r):
        source = lax.rem(my_slot + r, n_all)
        pltpu.make_async_remote_copy(
            src_ref=mine, dst_ref=slots.at[source], send_sem=q_send.at[r - 1], recv_sem=q_recv.at[source],
            device_id=place(source), device_id_type=MESH).wait_recv()

    for_peers(lambda r: report(r).start())

    with mark("drain"):
        for j in range(splits):
            loop(1, n_ma, lambda q: send(lax.rem(ma + q, n_ma), j).wait_send(), few)

            def passed(source):
                for q in range(1, n_pol):
                    hop(source, j, q, part(source, pol, j)).wait_send()
            loop(0, n_ma, passed, few)
    with mark("heard"):
        for_peers(heard)

    per_freq = n_ma * n_pol
    masked, live, here = 0.0, 0.0, 0.0
    for f in range(n_freq):
        channel = jnp.sum(jnp.sum(slots[f * per_freq:(f + 1) * per_freq, 0, :], axis=0, keepdims=True), axis=1, keepdims=True) / total
        flag = slots[f * per_freq, 1:2, 0:1]
        masked += flag * channel
        live += flag
        here += jnp.where(freq == f, channel, 0.0)
    band = masked / live
    factor = mine[1:2, 0:1] / jnp.sqrt(0.5 * here + 0.5 * band + 1e-06)
    power_ref[...] = jnp.broadcast_to(here, power_ref.shape)
    scale_ref[...] = rs_n[...] * factor
    for_peers(lambda r: report(r).wait_send())


def rescale_kernel(acc, scale_ref, power_ref, out_ref, channel_ref, staged, channel, sems, channel_sem):
    modes = scale_ref.shape[0]
    columns = acc.shape[1]
    strip = modes // sems.shape[0]
    channel[0] = power_ref[0, 0]
    last = pltpu.make_async_copy(channel, channel_ref, channel_sem)
    copies = []
    for i in range(sems.shape[0]):
        k0 = i * strip
        scale = scale_ref[k0:k0 + strip, :]
        for c in range(2):
            for j in range(columns // LANES):
                value = acc[c * modes + k0:c * modes + k0 + strip, j * LANES:(j + 1) * LANES]
                staged[c, k0:k0 + strip, j * LANES:(j + 1) * LANES] = (value * scale).astype(staged.dtype)
        copies.append(pltpu.make_async_copy(
            staged.at[:, pl.ds(k0, strip)], out_ref.at[:, pl.ds(k0, strip)], sems.at[i]))
        copies[-1].start()
        if i == 0:
            last.start()
    for copy in copies:
        copy.wait()
    last.wait()


def on_device(sizes, alm, beam, m_table, chan_mask, noise):
    n_ma, n_freq, n_pol = sizes
    coeffs = alm[:, 0]
    response = beam[0, 0]
    block, columns = coeffs.shape[1], coeffs.shape[3]
    modes, degrees = response.shape[1], response.shape[2]
    per_source = n_pol * block
    rows = per_source * max(1, min(n_ma, 256 // per_source))
    groups = degrees // rows
    splits = columns // LANES
    n_all = n_ma * n_freq * n_pol
    total = float(n_ma * modes * n_pol * columns)
    vmem = pl.BlockSpec(memory_space=pltpu.VMEM)
    hbm = pl.BlockSpec(memory_space=pltpu.HBM)
    dma = pltpu.SemaphoreType.DMA
    keep = functools.partial(pltpu.with_memory_space_constraint, memory_space=pltpu.HBM)
    visibility, scale, power = pl.pallas_call(
        functools.partial(step_kernel, sizes, total),
        out_shape=(
            jax.ShapeDtypeStruct((2 * modes, columns), jnp.float32),
            jax.ShapeDtypeStruct((modes, LANES), jnp.float32),
            jax.ShapeDtypeStruct((1, LANES), jnp.float32),
        ),
        in_specs=[hbm, hbm, hbm, hbm, hbm],
        out_specs=(vmem, vmem, vmem),
        scratch_shapes=[
            pltpu.VMEM((2, block, n_ma, columns), jnp.bfloat16),
            pltpu.VMEM((n_ma, splits, 2, block, LANES), jnp.bfloat16),
            pltpu.VMEM((groups, splits, 2, rows, LANES), jnp.bfloat16),
            pltpu.VMEM((groups, 2 * modes, 2 * rows), jnp.bfloat16),
            pltpu.VMEM((2, modes, degrees), jnp.bfloat16),
            pltpu.VMEM((modes, LANES), jnp.float32),
            pltpu.VMEM((modes, LANES), jnp.float32),
            pltpu.VMEM((2, LANES), jnp.float32),
            pltpu.VMEM((n_all, 2, LANES), jnp.float32),
            pltpu.SMEM((1, 1), jnp.int32),
            pltpu.SMEM((1, 1), jnp.int32),
            pltpu.VMEM((1, modes), jnp.float32),
            dma((n_ma, splits)), dma((n_ma, splits)), dma((n_ma, splits)), dma((n_ma, splits)),
            dma((2, 2 if block % 32 == 0 else 1)), dma,
            dma((n_all,)), dma((n_all,)),
            pltpu.SemaphoreType.REGULAR((max(1, n_ma - 2),)), pltpu.SemaphoreType.REGULAR((2,)), dma((3,)),
        ],
        compiler_params=pltpu.CompilerParams(collective_id=0, has_side_effects=True, vmem_limit_bytes=40 * 1024 * 1024),
        name="driftscan_step",
    )(keep(coeffs), keep(response), m_table[None], chan_mask[None], keep(noise))
    pieces = 8 if modes % 128 == 0 else 1
    scaled, channel_power = pl.pallas_call(
        rescale_kernel,
        out_shape=(
            jax.ShapeDtypeStruct((2, modes, columns), jnp.bfloat16),
            jax.ShapeDtypeStruct((1,), jnp.float32),
        ),
        in_specs=[vmem, vmem, vmem],
        out_specs=(hbm, hbm),
        scratch_shapes=[pltpu.VMEM((2, modes, columns), jnp.bfloat16), pltpu.SMEM((1,), jnp.float32), dma((pieces,)), dma],
        compiler_params=pltpu.CompilerParams(vmem_limit_bytes=16 * 1024 * 1024),
        name="rescale",
    )(visibility, scale, power)
    return scaled[:, None, None], channel_power


def solution(mesh):
    sizes = (mesh.shape["ma"], mesh.shape["freq"], mesh.shape["pol"])
    return jax.shard_map(
        functools.partial(on_device, sizes),
        mesh=mesh,
        in_specs=(
            P(None, "freq", ("ma", "pol"), None, "sky"),
            P("ma", "freq", None, "pol", None),
            P("ma"),
            P("freq"),
            P("freq", "pol"),
        ),
        out_specs=(P(None, "freq", "ma", "pol", "sky"), P(("sky", "freq"))),
        check_vma=False,
    )
```

time: 42.5 us -> 38.1 us (0.90)
  Pallas kernels: 38.8 us -> 36 us
  local copies, waits for them, and re-layouts: 1.43 us -> 0 us
    pallas_call x1, Pallas kernels: 37.3 us -> 34.9 us  [on_device(): pl.pallas_call(functools.partial(step_kernel, sizes, total), out_shape=(j...]
    unnamed x5 -> x0, local copies, waits for them, and re-layouts: 1.43 us -> none
    pallas_call x1, Pallas kernels: 1.57 us -> 1.07 us  [on_device(): pl.pallas_call(rescale_kernel, out_shape=(jax.ShapeDtypeStruct((2, modes,...]
where the time goes in v1:
time: 38.1 us; the launch traced here: 37.9 us
  Pallas kernels  36 us (94%)
  between operations  1.93 us (5%)
    pallas_call x1, Pallas kernels, on_device(): pl.pallas_call(functools.partial(step_kernel, sizes, total), out_shape=(j...  34.9 us
    pallas_call x1, Pallas kernels, on_device(): pl.pallas_call(rescale_kernel, out_shape=(jax.ShapeDtypeStruct((2, modes,...  1.07 us

profile of v1, /device:TPU:0, one launch (start us, length us, event | category | flops | bytes accessed | tf_op | source)
XLA Modules:
  0.0 37.9 jit_solution(15608537934545702471)
XLA Ops:
  1.9 34.9 %driftscan_step.1 = (f32[1024,512]{1,0:T(8,128)S(1)}, f32[512,128]{1,0:T(8,128)S(1)}, f32[1,128]{1,0:T(1,128)S(1)}) custom-call(bf16[2,128,4,512]{3,2,1,0:T(4,128)(2,1)} %bitcast.10, bf16[2,512,1024]{2,1,0:T(8,128)(2,1)} %bitcast.9, s32[1,1]{1,0:T(1,128)} %bitcast.7.m_hbm, s32[1,1]{1,0:T(1,128)} %bitcast.8.mask_hbm, f32[1,512]{1,0:T(1,128)} %noise_hbm.1), custom_call_target="tpu_custom_call" | custom-call | tf_op jit(solution)/shard_map/driftscan_step/pallas_call | solution.py:374
  36.9 1.1 %rescale.1 = (bf16[2,512,512]{2,1,0:T(8,128)(2,1)}, f32[1]{0:T(128)}) custom-call(f32[1024,512]{1,0:T(8,128)S(1)} %get-tuple-element.7.acc, f32[512,128]{1,0:T(8,128)S(1)} %get-tuple-element.8.scale_ref, f32[1,128]{1,0:T(1,128)S(1)} %get-tuple-element.9.power_ref), custom_call_target="tpu_custom_call" | custom-call | tf_op jit(solution)/shard_map/rescale/pallas_call | solution.py:405

commit v2 on v1

v2 whole, which is shorter than its diff:
```python
import contextlib
import functools

import jax
import jax.numpy as jnp
from jax import lax
from jax.experimental import pallas as pl
from jax.experimental.pallas import tpu as pltpu
from jax.sharding import PartitionSpec as P

MESH = pl.DeviceIdType.MESH
LANES = 128


def mark(name):
    return contextlib.nullcontext()


def across(n, i):
    return n // 2 if 2 * i < n else n // 2 - 1


def processing_order(n, i):
    last = across(n, i)
    rest = sorted((j for j in range(n) if j not in (i, last)), key=lambda j: (-abs(j - i), j))
    return rest + ([last] if last != i else [])


def far_first(n, i):
    return sorted((j for j in range(n) if j != i), key=lambda j: (-abs(j - i), j != across(n, i), j))


def pick_by(me, values):
    pick = jnp.int32(values[0])
    for i in range(1, len(values)):
        pick = jnp.where(me == i, jnp.int32(values[i]), pick)
    return pick


def step_kernel(
    sizes, total, alm_hbm, beam_hbm, m_ref, mask_ref, noise_hbm, acc, scale_ref, power_ref,
    staged, planes, recv, wide, beam_v, inv_n, rs_n, mine, slots, noise_ref,
    z_send, z_far, z_last, d_send, p_send, p_far, p_last, in_sem, beam_sem, q_send, q_recv, edge, meet, small_sem,
):
    n_ma, n_freq, n_pol = sizes
    n_all = n_ma * n_freq * n_pol
    ma, freq, pol = lax.axis_index("ma"), lax.axis_index("freq"), lax.axis_index("pol")
    block = staged.shape[1]
    groups, splits, _, rows, lanes = recv.shape
    per_source = n_pol * block
    per_group = rows // per_source
    modes = beam_hbm.shape[1]
    my_slot = (freq * n_ma + ma) * n_pol + pol
    few = n_ma <= 8 and per_group == 1 and n_pol == 2 and block % LANES == 0

    def place(slot):
        return {"ma": lax.rem(slot // n_pol, n_ma), "freq": slot // (n_pol * n_ma), "pol": lax.rem(slot, n_pol)}

    def loop(low, high, body, unroll=False):
        if unroll:
            for r in range(low, high):
                body(r)
        else:
            lax.fori_loop(low, high, lambda r, _: (body(r), 0)[1], 0)

    def for_peers(body):
        loop(1, n_all, body, n_all <= 32)

    barrier = pltpu.get_barrier_semaphore()

    def tell(axis, me, n, sem):
        loop(1, n, lambda q: pl.semaphore_signal(
            sem, inc=1, device_id={axis: lax.rem(me + q, n)}, device_id_type=MESH), n <= 8)

    low = n_ma // 2
    below = ma < low
    inward, outward = jnp.where(below, ma + 1, ma - 1), jnp.where(below, ma - 1, ma + 1)
    is_hub = jnp.logical_or(ma == low - 1, ma == low)
    has_outward = jnp.logical_and(ma > 0, ma < n_ma - 1)

    def tell_line(there, sem):
        pl.semaphore_signal(sem, inc=1, device_id={"ma": there}, device_id_type=MESH)

    @pl.when(is_hub)
    def _():
        tell_line(inward, barrier)

    @pl.when(has_outward)
    def _():
        tell_line(outward, barrier)

    tell("pol", pol, n_pol, barrier)
    tell("freq", freq, n_freq, barrier)

    pieces = in_sem.shape[0]
    width = splits // pieces

    def columns_of(h):
        return pl.ds(h * width * lanes, width * lanes)

    loads = [pltpu.make_async_copy(alm_hbm.at[:, :, :, columns_of(h)], staged.at[:, :, :, columns_of(h)], in_sem.at[h])
             for h in range(pieces)]
    for load in loads:
        load.start()
    noise_copy = pltpu.make_async_copy(noise_hbm, noise_ref, small_sem)
    beam_copy = pltpu.make_async_copy(beam_hbm, beam_v, beam_sem)

    def part(source, core, j):
        start = lax.rem(source, per_group) * per_source + core * block
        return recv.at[source // per_group, j, :, pl.ds(pl.multiple_of(start, block), block)]

    with mark("barrier"):
        pl.semaphore_wait(barrier, 1 + n_pol - 1 + n_freq - 1)

    @pl.when(jnp.logical_not(jnp.logical_or(is_hub, has_outward)))
    def _():
        tell_line(inward, edge.at[0])

    step = min(block, 16)

    def turn(h):
        with mark("load"):
            loads[h].wait()
        for c in range(2):
            for e in range(0, block, step):
                turned = jnp.transpose(staged[c, e:e + step, :, columns_of(h)], (1, 0, 2))
                for j in range(width):
                    planes[:, h * width + j, c, e:e + step, :] = turned[:, :, j * lanes:(j + 1) * lanes]

    def push(src, dst, sent, got, where):
        pltpu.make_async_remote_copy(
            src_ref=src, dst_ref=dst, send_sem=sent, recv_sem=got, device_id=where, device_id_type=MESH).start()

    def send(target, j, sem):
        push(planes.at[target, j], part(ma, pol, j), z_send, sem, {"ma": target})

    def send_last(i, target, j):
        send(target, j, z_last.at[j])
        if j == splits - 1 and {i, target} == {low - 1, low}:
            @pl.when(pol == 0)
            def _():
                push(planes.at[target, j], part(ma, pol, j), d_send, p_last.at[j], {"ma": target, "pol": 1})

    def whole(source, core):
        start = lax.rem(source, per_group) * per_source + core * block
        return recv.at[source // per_group, :, :, pl.ds(pl.multiple_of(start, block), block)]

    def await_all(ref, sem):
        pltpu.make_async_copy(ref, ref, sem).wait()

    def relay(source, j, sent, got, src=None):
        for q in range(1, n_pol):
            push(part(source, pol, j) if src is None else src, part(source, pol, j), sent, got,
                 {"pol": lax.rem(pol + q, n_pol)})

    def relayed(source):
        for q in range(1, n_pol):
            await_all(whole(source, lax.rem(pol + q, n_pol)), p_far.at[source])

    def send_phase(phase):
        for i in range(n_ma):
            near = i + 1 if i < low else i - 1
            outer = range(0, i) if i < low else range(i + 1, n_ma)
            plan = [(t, j) for t in far_first(n_ma, i) for j in range(splits)]
            first = [(near, j) for j in range(width)]
            second = [(t, j) for t, j in plan if t in outer]
            now = (first, second, [step for step in plan if step not in first + second])[phase]
            if now:
                @pl.when(ma == i)
                def _():
                    for t, j in now:
                        if i == across(n_ma, t):
                            send_last(i, t, j)
                        else:
                            send(t, j, z_far.at[i])

    turn(0)
    if few:
        send_phase(0)
    for h in range(1, pieces):
        turn(h)
    noise_copy.start()
    beam_copy.start()

    with mark("edge0"):
        @pl.when(has_outward)
        def _():
            pl.semaphore_wait(edge.at[0], 1)

    @pl.when(is_hub)
    def _():
        tell_line(inward, edge.at[1])

    @pl.when(jnp.logical_and(has_outward, jnp.logical_not(is_hub)))
    def _():
        tell_line(inward, edge.at[0])

    if few:
        send_phase(1)
    with mark("edge1"):
        pl.semaphore_wait(edge.at[1], 1)

    @pl.when(has_outward)
    def _():
        tell_line(outward, edge.at[1])

    if few:
        send_phase(2)
    else:
        for j in range(splits):
            loop(1, n_ma, lambda q: send(lax.rem(ma + q, n_ma), j, z_far.at[ma]))

    for j in range(splits):
        relay(ma, j, p_send.at[0], p_far.at[ma], planes.at[ma, j])
        for c in range(2):
            part(ma, pol, j)[c] = planes[ma, j, c]

    noise_copy.wait()
    spread = jnp.transpose(jnp.broadcast_to(noise_ref[...], (LANES, modes)))
    inv_n[...] = 1.0 / spread
    rs_n[...] = lax.rsqrt(spread)
    mine[1:2, :] = jnp.full((1, LANES), mask_ref[0].astype(jnp.float32))
    beam_copy.wait()
    strip = min(modes, 128)

    def widen(i):
        k0 = pl.multiple_of(i * strip, strip)
        for g in range(groups):
            degree = lax.broadcasted_iota(jnp.int32, (strip, rows), 1) + g * rows
            keep = degree >= m_ref[0]
            zero = jnp.zeros((strip, rows), jnp.float32)
            b0 = jnp.where(keep, beam_v[0, pl.ds(k0, strip), g * rows:(g + 1) * rows].astype(jnp.float32), zero)
            b1 = jnp.where(keep, beam_v[1, pl.ds(k0, strip), g * rows:(g + 1) * rows].astype(jnp.float32), zero)
            wide[g, pl.ds(k0, strip), 0:rows] = b0.astype(wide.dtype)
            wide[g, pl.ds(k0, strip), rows:2 * rows] = (-b1).astype(wide.dtype)
            wide[g, pl.ds(modes + k0, strip), 0:rows] = b1.astype(wide.dtype)
            wide[g, pl.ds(modes + k0, strip), rows:2 * rows] = b0.astype(wide.dtype)

    with mark("widen"):
        loop(0, modes // strip, widen)
    tell("pol", pol, n_pol, meet.at[0])
    pl.semaphore_wait(meet.at[0], n_pol - 1)
    tell("freq", freq, n_freq, meet.at[1])
    pl.semaphore_wait(meet.at[1], n_freq - 1)

    tile = min(modes, 256)

    def add(g, first=False):
        x = jnp.concatenate([recv[g, j].reshape(2 * rows, lanes) for j in range(splits)], axis=1)

        def body(k0):
            value = jnp.dot(wide[g, pl.ds(k0, tile), :], x, preferred_element_type=jnp.float32)
            acc[pl.ds(k0, tile), :] = value if first else acc[pl.ds(k0, tile), :] + value

        for i in range(2 * modes // tile):
            body(i * tile)

    def half(g, j, core):
        start = pl.multiple_of(core * block, block)
        x = jnp.concatenate([recv[g, j, c, pl.ds(start, block), :] for c in range(2)], axis=0)

        def value(k0):
            left = jnp.concatenate([wide[g, k0:k0 + tile, pl.ds(pl.multiple_of(c * rows + start, block), block)]
                                    for c in range(2)], axis=1)
            return jnp.dot(left, x, preferred_element_type=jnp.float32)
        return value

    def add_to(j, product):
        for i in range(2 * modes // tile):
            acc[i * tile:(i + 1) * tile, j * lanes:(j + 1) * lanes] += product(i * tile)

    def finish(g, j, power, product=None):
        for i in range(2 * modes // tile):
            at = (slice(i * tile, (i + 1) * tile), slice(j * lanes, (j + 1) * lanes))
            value = acc[at]
            if product is not None:
                value = value + product(i * tile)
                acc[at] = value
            k0 = i * tile % modes
            weighted = value * value * inv_n[k0:k0 + tile, :]
            power = power + jnp.sum(weighted.reshape(tile // 8, 8, lanes), axis=0)
        return power

    power = jnp.zeros((8, lanes), jnp.float32)
    if few:
        order = [pick_by(ma, [processing_order(n_ma, i)[k] for i in range(n_ma)]) for k in range(n_ma - 1)]
        last, before = order[-1], ma

        def settle(source, first):
            with mark("relay"):
                relayed(source)
            with mark("add"):
                add(source, first)

        for k in range(n_ma - 2):
            with mark(f"wait{k}"):
                await_all(whole(order[k], pol), z_far.at[order[k]])
            for j in range(splits):
                relay(order[k], j, p_send.at[1], p_far.at[order[k]])
            settle(before, k == 0)
            before = order[k]
        end = splits - 1
        direct = jnp.logical_and(is_hub, pol == 0)
        for j in range(splits):
            with mark(f"last{j}"):
                await_all(part(last, pol, j), z_last.at[j])
            if j < end:
                relay(last, j, p_send.at[2], p_last.at[j])
            else:
                @pl.when(jnp.logical_not(direct))
                def _():
                    relay(last, end, d_send, p_last.at[end])
            if j == 0:
                settle(before, n_ma == 2)
            add_to(j, half(last, j, pol))
            if j > 0:
                with mark(f"hop{j - 1}"):
                    await_all(part(last, 1 - pol, j - 1), p_last.at[j - 1])
                power = finish(last, j - 1, power, half(last, j - 1, 1 - pol))
        with mark("hoplast"):
            await_all(part(last, 1 - pol, end), p_last.at[end])
        power = finish(last, end, power, half(last, end, 1 - pol))
    else:
        def pass_on(source):
            @pl.when(source != ma)
            def _():
                await_all(whole(source, pol), z_far.at[source])
                for j in range(splits):
                    relay(source, j, p_send.at[1], p_far.at[source])
        loop(0, n_ma, pass_on)
        loop(0, n_ma, relayed)
        for g in range(groups):
            add(g, g == 0)
        for j in range(splits):
            power = finish(None, j, power)

    row = jnp.sum(power, axis=0, keepdims=True)
    mine[0:1, :] = row
    slots[my_slot, 0:1, :] = row
    slots[my_slot, 1:2, :] = mine[1:2, :]

    def report(r):
        pltpu.make_async_remote_copy(
            src_ref=mine, dst_ref=slots.at[my_slot], send_sem=q_send, recv_sem=q_recv,
            device_id=place(lax.rem(my_slot + r, n_all)), device_id_type=MESH).start()

    for_peers(report)

    with mark("drain"):
        await_all(planes.at[pl.ds(0, n_ma - 1)], z_send)
        await_all(planes.at[0], p_send.at[0])
        if few:
            if n_ma > 2:
                await_all(planes.at[pl.ds(0, n_ma - 2)], p_send.at[1])
            await_all(planes.at[0, pl.ds(0, splits - 1)], p_send.at[2])
            await_all(planes.at[0, 0], d_send)
        else:
            await_all(planes.at[pl.ds(0, n_ma - 1)], p_send.at[1])
    with mark("heard"):
        await_all(slots.at[pl.ds(0, n_all - 1)], q_recv)

    per_freq = n_ma * n_pol
    tail = mark('tail'); tail.__enter__()
    masked, live, here = 0.0, 0.0, 0.0
    for f in range(n_freq):
        channel = jnp.sum(jnp.sum(slots[f * per_freq:(f + 1) * per_freq, 0, :], axis=0, keepdims=True), axis=1, keepdims=True) / total
        flag = slots[f * per_freq, 1:2, 0:1]
        masked += flag * channel
        live += flag
        here += jnp.where(freq == f, channel, 0.0)
    band = masked / live
    factor = mine[1:2, 0:1] / jnp.sqrt(0.5 * here + 0.5 * band + 1e-06)
    power_ref[...] = jnp.broadcast_to(here, power_ref.shape)
    scale_ref[...] = rs_n[...] * factor
    await_all(slots.at[pl.ds(0, n_all - 1)], q_send)
    tail.__exit__(None,None,None)


def rescale_kernel(acc, scale_ref, power_ref, out_ref, channel_ref, staged, channel, sems, channel_sem):
    modes = scale_ref.shape[0]
    columns = acc.shape[1]
    strip = modes // sems.shape[0]
    channel[0] = power_ref[0, 0]
    last = pltpu.make_async_copy(channel, channel_ref, channel_sem)
    copies = []
    for i in range(sems.shape[0]):
        k0 = i * strip
        scale = scale_ref[k0:k0 + strip, :]
        for c in range(2):
            for j in range(columns // LANES):
                value = acc[c * modes + k0:c * modes + k0 + strip, j * LANES:(j + 1) * LANES]
                staged[c, k0:k0 + strip, j * LANES:(j + 1) * LANES] = (value * scale).astype(staged.dtype)
        copies.append(pltpu.make_async_copy(
            staged.at[:, pl.ds(k0, strip)], out_ref.at[:, pl.ds(k0, strip)], sems.at[i]))
        copies[-1].start()
        if i == 0:
            last.start()
    for copy in copies:
        copy.wait()
    last.wait()


def on_device(sizes, alm, beam, m_table, chan_mask, noise):
    n_ma, n_freq, n_pol = sizes
    coeffs = alm[:, 0]
    response = beam[0, 0]
    block, columns = coeffs.shape[1], coeffs.shape[3]
    modes, degrees = response.shape[1], response.shape[2]
    per_source = n_pol * block
    rows = per_source * max(1, min(n_ma, 256 // per_source))
    groups = degrees // rows
    splits = columns // LANES
    n_all = n_ma * n_freq * n_pol
    total = float(n_ma * modes * n_pol * columns)
    vmem = pl.BlockSpec(memory_space=pltpu.VMEM)
    hbm = pl.BlockSpec(memory_space=pltpu.HBM)
    smem = pl.BlockSpec(memory_space=pltpu.SMEM)
    dma = pltpu.SemaphoreType.DMA
    keep = functools.partial(pltpu.with_memory_space_constraint, memory_space=pltpu.HBM)
    visibility, scale, power = pl.pallas_call(
        functools.partial(step_kernel, sizes, total),
        out_shape=(
            jax.ShapeDtypeStruct((2 * modes, columns), jnp.float32),
            jax.ShapeDtypeStruct((modes, LANES), jnp.float32),
            jax.ShapeDtypeStruct((1, LANES), jnp.float32),
        ),
        in_specs=[hbm, hbm, smem, smem, hbm],
        out_specs=(vmem, vmem, vmem),
        scratch_shapes=[
            pltpu.VMEM((2, block, n_ma, columns), jnp.bfloat16),
            pltpu.VMEM((n_ma, splits, 2, block, LANES), jnp.bfloat16),
            pltpu.VMEM((groups, splits, 2, rows, LANES), jnp.bfloat16),
            pltpu.VMEM((groups, 2 * modes, 2 * rows), jnp.bfloat16),
            pltpu.VMEM((2, modes, degrees), jnp.bfloat16),
            pltpu.VMEM((modes, LANES), jnp.float32),
            pltpu.VMEM((modes, LANES), jnp.float32),
            pltpu.VMEM((2, LANES), jnp.float32),
            pltpu.VMEM((n_all, 2, LANES), jnp.float32),
            pltpu.VMEM((1, modes), jnp.float32),
            dma, dma((n_ma,)), dma((splits,)), dma, dma((3,)), dma((n_ma,)), dma((splits,)),
            dma((2 if splits % 2 == 0 else 1,)), dma, dma, dma,
            pltpu.SemaphoreType.REGULAR((2,)), pltpu.SemaphoreType.REGULAR((2,)), dma,
        ],
        compiler_params=pltpu.CompilerParams(collective_id=0, has_side_effects=True, vmem_limit_bytes=40 * 1024 * 1024),
        name="driftscan_step",
    )(keep(coeffs), keep(response), m_table, chan_mask, keep(noise))
    pieces = 8 if modes % 128 == 0 else 1
    scaled, channel_power = pl.pallas_call(
        rescale_kernel,
        out_shape=(
            jax.ShapeDtypeStruct((2, modes, columns), jnp.bfloat16),
            jax.ShapeDtypeStruct((1,), jnp.float32),
        ),
        in_specs=[vmem, vmem, vmem],
        out_specs=(hbm, hbm),
        scratch_shapes=[pltpu.VMEM((2, modes, columns), jnp.bfloat16), pltpu.SMEM((1,), jnp.float32), dma((pieces,)), dma],
        compiler_params=pltpu.CompilerParams(vmem_limit_bytes=16 * 1024 * 1024),
        name="rescale",
    )(visibility, scale, power)
    return scaled[:, None, None], channel_power


def solution(mesh):
    sizes = (mesh.shape["ma"], mesh.shape["freq"], mesh.shape["pol"])
    return jax.shard_map(
        functools.partial(on_device, sizes),
        mesh=mesh,
        in_specs=(
            P(None, "freq", ("ma", "pol"), None, "sky"),
            P("ma", "freq", None, "pol", None),
            P("ma"),
            P("freq"),
            P("freq", "pol"),
        ),
        out_specs=(P(None, "freq", "ma", "pol", "sky"), P(("sky", "freq"))),
        check_vma=False,
    )
```

time: 38.1 us -> 36.2 us (0.950)
  Pallas kernels: 36 us -> 34.1 us
    pallas_call x1, Pallas kernels: 34.9 us -> 33 us  [on_device(): pl.pallas_call(functools.partial(step_kernel, sizes, total), out_shape=(j...]
where the time goes in v2:
time: 36.2 us; the launch traced here: 36 us
  Pallas kernels  34.1 us (94%)
  between operations  1.93 us (5%)
    pallas_call x1, Pallas kernels, on_device(): pl.pallas_call(functools.partial(step_kernel, sizes, total), out_shape=(j...  33 us
    pallas_call x1, Pallas kernels, on_device(): pl.pallas_call(rescale_kernel, out_shape=(jax.ShapeDtypeStruct((2, modes,...  1.07 us

profile of v2, /device:TPU:0, one launch (start us, length us, event | category | flops | bytes accessed | tf_op | source)
XLA Modules:
  0.0 36.0 jit_solution(1255795045962819969)
XLA Ops:
  1.9 33.0 %driftscan_step.1 = (f32[1024,512]{1,0:T(8,128)S(1)}, f32[512,128]{1,0:T(8,128)S(1)}, f32[1,128]{1,0:T(1,128)S(1)}) custom-call(bf16[2,128,4,512]{3,2,1,0:T(4,128)(2,1)} %bitcast.6, bf16[2,512,1024]{2,1,0:T(8,128)(2,1)} %bitcast.5, s32[1]{0:T(128)S(6)} %copy.8.m_ref, s32[1]{0:T(128)S(6)} %copy.9.mask_ref, f32[1,512]{1,0:T(1,128)} %noise_hbm.1), custom_call_target="tpu_custom_call" | custom-call | tf_op jit(solution)/shard_map/driftscan_step/pallas_call | solution.py:420
  35.0 1.1 %rescale.1 = (bf16[2,512,512]{2,1,0:T(8,128)(2,1)}, f32[1]{0:T(128)}) custom-call(f32[1024,512]{1,0:T(8,128)S(1)} %get-tuple-element.7.acc, f32[512,128]{1,0:T(8,128)S(1)} %get-tuple-element.8.scale_ref, f32[1,128]{1,0:T(1,128)S(1)} %get-tuple-element.9.power_ref), custom_call_target="tpu_custom_call" | custom-call | tf_op jit(solution)/shard_map/rescale/pallas_call | solution.py:448

commit v3 on v2

--- a/solution.py
+++ b/solution.py
@@ -39,7 +39,7 @@
 
 def step_kernel(
     sizes, total, alm_hbm, beam_hbm, m_ref, mask_ref, noise_hbm, acc, scale_ref, power_ref,
-    staged, planes, recv, wide, beam_v, inv_n, rs_n, mine, slots, noise_ref,
+    staged, planes, recv, wide, beam_v, inv_n, rs_n, mine, slots, total_ref, noise_ref,
     z_send, z_far, z_last, d_send, p_send, p_far, p_last, in_sem, beam_sem, q_send, q_recv, edge, meet, small_sem,
 ):
     n_ma, n_freq, n_pol = sizes
@@ -51,7 +51,7 @@
     per_group = rows // per_source
     modes = beam_hbm.shape[1]
     my_slot = (freq * n_ma + ma) * n_pol + pol
-    few = n_ma <= 8 and per_group == 1 and n_pol == 2 and block % LANES == 0
+    few = n_ma <= 8 and per_group == 1 and n_pol == 2 and block % LANES == 0 and splits > 1
 
     def place(slot):
         return {"ma": lax.rem(slot // n_pol, n_ma), "freq": slot // (n_pol * n_ma), "pol": lax.rem(slot, n_pol)}
@@ -92,14 +92,11 @@
     tell("pol", pol, n_pol, barrier)
     tell("freq", freq, n_freq, barrier)
 
-    pieces = in_sem.shape[0]
-    width = splits // pieces
-
-    def columns_of(h):
-        return pl.ds(h * width * lanes, width * lanes)
-
-    loads = [pltpu.make_async_copy(alm_hbm.at[:, :, :, columns_of(h)], staged.at[:, :, :, columns_of(h)], in_sem.at[h])
-             for h in range(pieces)]
+    def columns_of(j):
+        return pl.ds(j * lanes, lanes)
+
+    loads = [pltpu.make_async_copy(alm_hbm.at[:, :, :, columns_of(j)], staged.at[:, :, :, columns_of(j)], in_sem.at[j])
+             for j in range(splits)]
     for load in loads:
         load.start()
     noise_copy = pltpu.make_async_copy(noise_hbm, noise_ref, small_sem)
@@ -109,23 +106,30 @@
         start = lax.rem(source, per_group) * per_source + core * block
         return recv.at[source // per_group, j, :, pl.ds(pl.multiple_of(start, block), block)]
 
-    with mark("barrier"):
+    is_end = jnp.logical_not(jnp.logical_or(is_hub, has_outward))
+
+    def enter():
         pl.semaphore_wait(barrier, 1 + n_pol - 1 + n_freq - 1)
 
-    @pl.when(jnp.logical_not(jnp.logical_or(is_hub, has_outward)))
+    @pl.when(is_end)
     def _():
+        enter()
         tell_line(inward, edge.at[0])
 
     step = min(block, 16)
 
-    def turn(h):
+    def turn(j):
         with mark("load"):
-            loads[h].wait()
+            loads[j].wait()
         for c in range(2):
             for e in range(0, block, step):
-                turned = jnp.transpose(staged[c, e:e + step, :, columns_of(h)], (1, 0, 2))
-                for j in range(width):
-                    planes[:, h * width + j, c, e:e + step, :] = turned[:, :, j * lanes:(j + 1) * lanes]
+                planes[:, j, c, e:e + step, :] = jnp.transpose(staged[c, e:e + step, :, columns_of(j)], (1, 0, 2))
+
+    turn(0)
+    with mark("barrier"):
+        @pl.when(jnp.logical_not(is_end))
+        def _():
+            enter()
 
     def push(src, dst, sent, got, where):
         pltpu.make_async_remote_copy(
@@ -162,9 +166,10 @@
             near = i + 1 if i < low else i - 1
             outer = range(0, i) if i < low else range(i + 1, n_ma)
             plan = [(t, j) for t in far_first(n_ma, i) for j in range(splits)]
-            first = [(near, j) for j in range(width)]
+            first = [(near, j) for j in range(min(2, splits))]
             second = [(t, j) for t, j in plan if t in outer]
-            now = (first, second, [step for step in plan if step not in first + second])[phase]
+            rest = [step for step in plan if step not in first + second]
+            now = (first[:1], first[1:], second, rest)[phase]
             if now:
                 @pl.when(ma == i)
                 def _():
@@ -174,11 +179,12 @@
                         else:
                             send(t, j, z_far.at[i])
 
-    turn(0)
     if few:
         send_phase(0)
-    for h in range(1, pieces):
-        turn(h)
+    for j in range(1, splits):
+        turn(j)
+        if few and j == 1:
+            send_phase(1)
     noise_copy.start()
     beam_copy.start()
 
@@ -196,7 +202,7 @@
         tell_line(inward, edge.at[0])
 
     if few:
-        send_phase(1)
+        send_phase(2)
     with mark("edge1"):
         pl.semaphore_wait(edge.at[1], 1)
 
@@ -205,7 +211,7 @@
         tell_line(outward, edge.at[1])
 
     if few:
-        send_phase(2)
+        send_phase(3)
     else:
         for j in range(splits):
             loop(1, n_ma, lambda q: send(lax.rem(ma + q, n_ma), j, z_far.at[ma]))
@@ -255,9 +261,10 @@
         for i in range(2 * modes // tile):
             body(i * tile)
 
-    def half(g, j, core):
+    def half(g, first, end, core):
         start = pl.multiple_of(core * block, block)
-        x = jnp.concatenate([recv[g, j, c, pl.ds(start, block), :] for c in range(2)], axis=0)
+        x = jnp.concatenate([jnp.concatenate([recv[g, j, c, pl.ds(start, block), :] for c in range(2)], axis=0)
+                             for j in range(first, end)], axis=1)
 
         def value(k0):
             left = jnp.concatenate([wide[g, k0:k0 + tile, pl.ds(pl.multiple_of(c * rows + start, block), block)]
@@ -269,19 +276,26 @@
         for i in range(2 * modes // tile):
             acc[i * tile:(i + 1) * tile, j * lanes:(j + 1) * lanes] += product(i * tile)
 
-    def finish(g, j, power, product=None):
+    def full(g, j):
+        x = recv[g, j].reshape(2 * rows, lanes)
+        return lambda k0: jnp.dot(wide[g, k0:k0 + tile, :], x, preferred_element_type=jnp.float32)
+
+    def finish(first, end, product=None):
+        power = total_ref[...]
         for i in range(2 * modes // tile):
-            at = (slice(i * tile, (i + 1) * tile), slice(j * lanes, (j + 1) * lanes))
+            at = (slice(i * tile, (i + 1) * tile), slice(first * lanes, end * lanes))
             value = acc[at]
             if product is not None:
                 value = value + product(i * tile)
                 acc[at] = value
             k0 = i * tile % modes
-            weighted = value * value * inv_n[k0:k0 + tile, :]
-            power = power + jnp.sum(weighted.reshape(tile // 8, 8, lanes), axis=0)
-        return power
-
-    power = jnp.zeros((8, lanes), jnp.float32)
+            weights = inv_n[k0:k0 + tile, :]
+            for j in range(end - first):
+                one = value[:, j * lanes:(j + 1) * lanes]
+                power = power + jnp.sum((one * one * weights).reshape(tile // 8, 8, lanes), axis=0)
+        total_ref[...] = power
+
+    total_ref[...] = jnp.zeros_like(total_ref)
     if few:
         order = [pick_by(ma, [processing_order(n_ma, i)[k] for i in range(n_ma)]) for k in range(n_ma - 1)]
         last, before = order[-1], ma
@@ -301,25 +315,42 @@
             before = order[k]
         end = splits - 1
         direct = jnp.logical_and(is_hub, pol == 0)
-        for j in range(splits):
+
+        def own_block(j):
             with mark(f"last{j}"):
                 await_all(part(last, pol, j), z_last.at[j])
-            if j < end:
-                relay(last, j, p_send.at[2], p_last.at[j])
-            else:
-                @pl.when(jnp.logical_not(direct))
-                def _():
-                    relay(last, end, d_send, p_last.at[end])
-            if j == 0:
-                settle(before, n_ma == 2)
-            add_to(j, half(last, j, pol))
-            if j > 0:
-                with mark(f"hop{j - 1}"):
-                    await_all(part(last, 1 - pol, j - 1), p_last.at[j - 1])
-                power = finish(last, j - 1, power, half(last, j - 1, 1 - pol))
-        with mark("hoplast"):
-            await_all(part(last, 1 - pol, end), p_last.at[end])
-        power = finish(last, end, power, half(last, end, 1 - pol))
+
+        def other_block(j):
+            with mark(f"hop{j}"):
+                await_all(part(last, 1 - pol, j), p_last.at[j])
+
+        own_block(0)
+        relay(last, 0, p_send.at[2], p_last.at[0])
+        settle(before, n_ma == 2)
+
+        @pl.when(direct)
+        def _():
+            for j in range(splits):
+                if j > 0:
+                    own_block(j)
+                    if j < end:
+                        relay(last, j, p_send.at[2], p_last.at[j])
+                other_block(j)
+                finish(j, j + 1, full(last, j))
+
+        @pl.when(jnp.logical_not(direct))
+        def _():
+            for j in range(splits):
+                if j > 0:
+                    own_block(j)
+                    relay(last, j, p_send.at[2] if j < end else d_send, p_last.at[j])
+                add_to(j, half(last, j, j + 1, pol))
+                if 0 < j < end:
+                    other_block(j - 1)
+                    finish(j - 1, j, half(last, j - 1, j, 1 - pol))
+            other_block(end - 1)
+            other_block(end)
+            finish(end - 1, splits, half(last, end - 1, splits, 1 - pol))
     else:
         def pass_on(source):
             @pl.when(source != ma)
@@ -332,9 +363,9 @@
         for g in range(groups):
             add(g, g == 0)
         for j in range(splits):
-            power = finish(None, j, power)
-
-    row = jnp.sum(power, axis=0, keepdims=True)
+            finish(j, j + 1)
+
+    row = jnp.sum(total_ref[...], axis=0, keepdims=True)
     mine[0:1, :] = row
     slots[my_slot, 0:1, :] = row
     slots[my_slot, 1:2, :] = mine[1:2, :]
@@ -436,9 +467,10 @@
             pltpu.VMEM((modes, LANES), jnp.float32),
             pltpu.VMEM((2, LANES), jnp.float32),
             pltpu.VMEM((n_all, 2, LANES), jnp.float32),
+            pltpu.VMEM((8, LANES), jnp.float32),
             pltpu.VMEM((1, modes), jnp.float32),
             dma, dma((n_ma,)), dma((splits,)), dma, dma((3,)), dma((n_ma,)), dma((splits,)),
-            dma((2 if splits % 2 == 0 else 1,)), dma, dma, dma,
+            dma((splits,)), dma, dma, dma,
             pltpu.SemaphoreType.REGULAR((2,)), pltpu.SemaphoreType.REGULAR((2,)), dma,
         ],
         compiler_params=pltpu.CompilerParams(collective_id=0, has_side_effects=True, vmem_limit_bytes=40 * 1024 * 1024),

time: 36.2 us -> 35.7 us (0.986)
  Pallas kernels: 34.1 us -> 33.5 us
    pallas_call x1, Pallas kernels: 33 us -> 32.5 us  [on_device(): pl.pallas_call(functools.partial(step_kernel, sizes, total), out_shape=(j...]
where the time goes in v3:
time: 35.7 us; the launch traced here: 35.5 us
  Pallas kernels  33.5 us (94%)
  between operations  1.93 us (5%)
    pallas_call x1, Pallas kernels, on_device(): pl.pallas_call(functools.partial(step_kernel, sizes, total), out_shape=(j...  32.5 us
    pallas_call x1, Pallas kernels, on_device(): pl.pallas_call(rescale_kernel, out_shape=(jax.ShapeDtypeStruct((2, modes,...  1.07 us

profile of v3, /device:TPU:0, one launch (start us, length us, event | category | flops | bytes accessed | tf_op | source)
XLA Modules:
  0.0 35.5 jit_solution(5076916520318241940)
XLA Ops:
  1.9 32.5 %driftscan_step.1 = (f32[1024,512]{1,0:T(8,128)S(1)}, f32[512,128]{1,0:T(8,128)S(1)}, f32[1,128]{1,0:T(1,128)S(1)}) custom-call(bf16[2,128,4,512]{3,2,1,0:T(4,128)(2,1)} %bitcast.6, bf16[2,512,1024]{2,1,0:T(8,128)(2,1)} %bitcast.5, s32[1]{0:T(128)S(6)} %copy.8.m_ref, s32[1]{0:T(128)S(6)} %copy.9.mask_ref, f32[1,512]{1,0:T(1,128)} %noise_hbm.1), custom_call_target="tpu_custom_call" | custom-call | tf_op jit(solution)/shard_map/driftscan_step/pallas_call | solution.py:451
  34.4 1.1 %rescale.1 = (bf16[2,512,512]{2,1,0:T(8,128)(2,1)}, f32[1]{0:T(128)}) custom-call(f32[1024,512]{1,0:T(8,128)S(1)} %get-tuple-element.7.acc, f32[512,128]{1,0:T(8,128)S(1)} %get-tuple-element.8.scale_ref, f32[1,128]{1,0:T(1,128)S(1)} %get-tuple-element.9.power_ref), custom_call_target="tpu_custom_call" | custom-call | tf_op jit(solution)/shard_map/rescale/pallas_call | solution.py:480

commit v4 on v3

--- a/solution.py
+++ b/solution.py
@@ -39,8 +39,9 @@
 
 def step_kernel(
     sizes, total, alm_hbm, beam_hbm, m_ref, mask_ref, noise_hbm, acc, scale_ref, power_ref,
-    staged, planes, recv, wide, beam_v, inv_n, rs_n, mine, slots, total_ref, noise_ref,
-    z_send, z_far, z_last, d_send, p_send, p_far, p_last, in_sem, beam_sem, q_send, q_recv, edge, meet, small_sem,
+    staged, planes, extra, recv, wide, wide_o, beam_v, beam_o, acc_o, incoming, inv_n, inv_o, rs_n, mine, slots, total_ref,
+    noise_ref, noise_o,
+    z_send, near_send, x_send, x_recv, b_send, b_recv, i_send, i_recv, z_far, z_last, y_last, p_send, p_far, p_last, in_sem, beam_sem, q_send, q_recv, edge, meet, small_sem,
 ):
     n_ma, n_freq, n_pol = sizes
     n_all = n_ma * n_freq * n_pol
@@ -51,7 +52,7 @@
     per_group = rows // per_source
     modes = beam_hbm.shape[1]
     my_slot = (freq * n_ma + ma) * n_pol + pol
-    few = n_ma <= 8 and per_group == 1 and n_pol == 2 and block % LANES == 0 and splits > 1
+    few = 2 < n_ma <= 8 and per_group == 1 and n_pol == 2 and block % LANES == 0 and splits > 3
 
     def place(slot):
         return {"ma": lax.rem(slot // n_pol, n_ma), "freq": slot // (n_pol * n_ma), "pol": lax.rem(slot, n_pol)}
@@ -77,6 +78,7 @@
     inward, outward = jnp.where(below, ma + 1, ma - 1), jnp.where(below, ma - 1, ma + 1)
     is_hub = jnp.logical_or(ma == low - 1, ma == low)
     has_outward = jnp.logical_and(ma > 0, ma < n_ma - 1)
+    hub_lead, hub_other = jnp.logical_and(is_hub, pol == 1), jnp.logical_and(is_hub, pol == 0)
 
     def tell_line(there, sem):
         pl.semaphore_signal(sem, inc=1, device_id={"ma": there}, device_id_type=MESH)
@@ -135,15 +137,8 @@
         pltpu.make_async_remote_copy(
             src_ref=src, dst_ref=dst, send_sem=sent, recv_sem=got, device_id=where, device_id_type=MESH).start()
 
-    def send(target, j, sem):
-        push(planes.at[target, j], part(ma, pol, j), z_send, sem, {"ma": target})
-
-    def send_last(i, target, j):
-        send(target, j, z_last.at[j])
-        if j == splits - 1 and {i, target} == {low - 1, low}:
-            @pl.when(pol == 0)
-            def _():
-                push(planes.at[target, j], part(ma, pol, j), d_send, p_last.at[j], {"ma": target, "pol": 1})
+    def send(target, j, got, sent):
+        push(planes.at[target, j], part(ma, pol, j), sent, got, {"ma": target})
 
     def whole(source, core):
         start = lax.rem(source, per_group) * per_source + core * block
@@ -160,24 +155,38 @@
     def relayed(source):
         for q in range(1, n_pol):
             await_all(whole(source, lax.rem(pol + q, n_pol)), p_far.at[source])
+
+    held = splits - 2
 
     def send_phase(phase):
         for i in range(n_ma):
             near = i + 1 if i < low else i - 1
             outer = range(0, i) if i < low else range(i + 1, n_ma)
             plan = [(t, j) for t in far_first(n_ma, i) for j in range(splits)]
-            first = [(near, j) for j in range(min(2, splits))]
+            first = [(near, j) for j in range(2)]
             second = [(t, j) for t, j in plan if t in outer]
             rest = [step for step in plan if step not in first + second]
+            hub = i in (low - 1, low)
             now = (first[:1], first[1:], second, rest)[phase]
+            late = [(t, j) for t, j in now if hub and t == near and j >= held]
             if now:
                 @pl.when(ma == i)
                 def _():
                     for t, j in now:
-                        if i == across(n_ma, t):
-                            send_last(i, t, j)
-                        else:
-                            send(t, j, z_far.at[i])
+                        if (t, j) not in late:
+                            send(t, j, z_last.at[j] if i == across(n_ma, t) else z_far.at[i],
+                                 near_send if t == near else z_send)
+                    if late:
+                        @pl.when(pol == 0)
+                        def _():
+                            push(planes.at[near, pl.ds(held, 2)], extra, near_send, x_recv, {"pol": 1})
+
+                        @pl.when(pol == 1)
+                        def _():
+                            await_all(extra, x_recv)
+                            for t, j in late:
+                                push(extra.at[j - held], part(ma, 0, j), x_send, y_last.at[j - held], {"ma": t})
+                                send(t, j, z_last.at[j], near_send)
 
     if few:
         send_phase(0)
@@ -214,12 +223,18 @@
         send_phase(3)
     else:
         for j in range(splits):
-            loop(1, n_ma, lambda q: send(lax.rem(ma + q, n_ma), j, z_far.at[ma]))
+            loop(1, n_ma, lambda q: send(lax.rem(ma + q, n_ma), j, z_far.at[ma], z_send))
 
     for j in range(splits):
         relay(ma, j, p_send.at[0], p_far.at[ma], planes.at[ma, j])
         for c in range(2):
             part(ma, pol, j)[c] = planes[ma, j, c]
+
+    if few:
+        @pl.when(hub_other)
+        def _():
+            push(beam_hbm, beam_o, b_send.at[0], b_recv.at[0], {"pol": 1})
+            push(noise_hbm, noise_o, b_send.at[1], b_recv.at[1], {"pol": 1})
 
     noise_copy.wait()
     spread = jnp.transpose(jnp.broadcast_to(noise_ref[...], (LANES, modes)))
@@ -229,7 +244,7 @@
     beam_copy.wait()
     strip = min(modes, 128)
 
-    def widen(i):
+    def widen(beam_v, wide, i):
         k0 = pl.multiple_of(i * strip, strip)
         for g in range(groups):
             degree = lax.broadcasted_iota(jnp.int32, (strip, rows), 1) + g * rows
@@ -243,12 +258,20 @@
             wide[g, pl.ds(modes + k0, strip), rows:2 * rows] = b0.astype(wide.dtype)
 
     with mark("widen"):
-        loop(0, modes // strip, widen)
+        loop(0, modes // strip, functools.partial(widen, beam_v, wide))
     tell("pol", pol, n_pol, meet.at[0])
     pl.semaphore_wait(meet.at[0], n_pol - 1)
     tell("freq", freq, n_freq, meet.at[1])
     pl.semaphore_wait(meet.at[1], n_freq - 1)
 
+    if few:
+        @pl.when(hub_lead)
+        def _():
+            await_all(noise_o, b_recv.at[1])
+            inv_o[...] = 1.0 / jnp.transpose(jnp.broadcast_to(noise_o[...], (LANES, modes)))
+            await_all(beam_o, b_recv.at[0])
+            loop(0, modes // strip, functools.partial(widen, beam_o, wide_o))
+
     tile = min(modes, 256)
 
     def add(g, first=False):
@@ -261,96 +284,144 @@
         for i in range(2 * modes // tile):
             body(i * tile)
 
-    def half(g, first, end, core):
+    def half(w, g, j, core):
         start = pl.multiple_of(core * block, block)
-        x = jnp.concatenate([jnp.concatenate([recv[g, j, c, pl.ds(start, block), :] for c in range(2)], axis=0)
-                             for j in range(first, end)], axis=1)
+        x = jnp.concatenate([recv[g, j, c, pl.ds(start, block), :] for c in range(2)], axis=0)
 
         def value(k0):
-            left = jnp.concatenate([wide[g, k0:k0 + tile, pl.ds(pl.multiple_of(c * rows + start, block), block)]
+            left = jnp.concatenate([w[g, k0:k0 + tile, pl.ds(pl.multiple_of(c * rows + start, block), block)]
                                     for c in range(2)], axis=1)
             return jnp.dot(left, x, preferred_element_type=jnp.float32)
         return value
 
-    def add_to(j, product):
+    def full(w, g, j):
+        x = recv[g, j].reshape(2 * rows, lanes)
+        return lambda k0: jnp.dot(w[g, k0:k0 + tile, :], x, preferred_element_type=jnp.float32)
+
+    def add_to(sums, j, product, first=False):
         for i in range(2 * modes // tile):
-            acc[i * tile:(i + 1) * tile, j * lanes:(j + 1) * lanes] += product(i * tile)
-
-    def full(g, j):
-        x = recv[g, j].reshape(2 * rows, lanes)
-        return lambda k0: jnp.dot(wide[g, k0:k0 + tile, :], x, preferred_element_type=jnp.float32)
-
-    def finish(first, end, product=None):
+            at = (slice(i * tile, (i + 1) * tile), slice(j * lanes, (j + 1) * lanes))
+            sums[at] = product(i * tile) if first else sums[at] + product(i * tile)
+
+    def finish(sums, weights, j, product=None):
         power = total_ref[...]
         for i in range(2 * modes // tile):
-            at = (slice(i * tile, (i + 1) * tile), slice(first * lanes, end * lanes))
-            value = acc[at]
+            at = (slice(i * tile, (i + 1) * tile), slice(j * lanes, (j + 1) * lanes))
+            value = sums[at]
             if product is not None:
                 value = value + product(i * tile)
-                acc[at] = value
+                sums[at] = value
             k0 = i * tile % modes
-            weights = inv_n[k0:k0 + tile, :]
-            for j in range(end - first):
-                one = value[:, j * lanes:(j + 1) * lanes]
-                power = power + jnp.sum((one * one * weights).reshape(tile // 8, 8, lanes), axis=0)
+            weighted = value * value * weights[k0:k0 + tile, :]
+            power = power + jnp.sum(weighted.reshape(tile // 8, 8, lanes), axis=0)
         total_ref[...] = power
 
+    def finish_both(product, product_o):
+        power, power_o = total_ref[...], jnp.zeros(total_ref.shape, jnp.float32)
+        for i in range(2 * modes // tile):
+            row, k0 = slice(i * tile, (i + 1) * tile), i * tile % modes
+            value_o = acc_o[row, :] + product_o(i * tile)
+            value = acc[row, (splits - 1) * lanes:] + product(i * tile)
+            acc_o[row, :] = value_o
+            acc[row, (splits - 1) * lanes:] = value
+            power_o = power_o + jnp.sum((value_o * value_o * inv_o[k0:k0 + tile, :]).reshape(tile // 8, 8, lanes), axis=0)
+            power = power + jnp.sum((value * value * inv_n[k0:k0 + tile, :]).reshape(tile // 8, 8, lanes), axis=0)
+        total_ref[...] = power + power_o
+
     total_ref[...] = jnp.zeros_like(total_ref)
     if few:
         order = [pick_by(ma, [processing_order(n_ma, i)[k] for i in range(n_ma)]) for k in range(n_ma - 1)]
-        last, before = order[-1], ma
-
-        def settle(source, first):
+        last, end = order[-1], splits - 1
+
+        def own_block(j):
+            with mark(f"last{j}"):
+                await_all(part(last, pol, j), z_last.at[j])
+
+        def other_block(j):
+            with mark(f"hop{j}"):
+                await_all(part(last, 1 - pol, j), p_last.at[j])
+
+        def pass_block(j, core=None, slot=None):
+            at = part(last, pol if core is None else core, j)
+            push(at, at, p_send.at[2], p_last.at[j if slot is None else slot], {"pol": 1 - pol})
+
+        def take(k):
+            with mark(f"wait{k}"):
+                await_all(whole(order[k], pol), z_far.at[order[k]])
+            for j in range(splits):
+                relay(order[k], j, p_send.at[1], p_far.at[order[k]])
+
+        def settle(source, first=False, shared=False):
             with mark("relay"):
                 relayed(source)
             with mark("add"):
                 add(source, first)
-
-        for k in range(n_ma - 2):
-            with mark(f"wait{k}"):
-                await_all(whole(order[k], pol), z_far.at[order[k]])
-            for j in range(splits):
-                relay(order[k], j, p_send.at[1], p_far.at[order[k]])
-            settle(before, k == 0)
-            before = order[k]
-        end = splits - 1
-        direct = jnp.logical_and(is_hub, pol == 0)
-
-        def own_block(j):
-            with mark(f"last{j}"):
-                await_all(part(last, pol, j), z_last.at[j])
-
-        def other_block(j):
-            with mark(f"hop{j}"):
-                await_all(part(last, 1 - pol, j), p_last.at[j])
-
-        own_block(0)
-        relay(last, 0, p_send.at[2], p_last.at[0])
-        settle(before, n_ma == 2)
-
-        @pl.when(direct)
-        def _():
-            for j in range(splits):
-                if j > 0:
-                    own_block(j)
-                    if j < end:
-                        relay(last, j, p_send.at[2], p_last.at[j])
+                if shared:
+                    @pl.when(hub_lead)
+                    def _():
+                        add_to(acc_o, 0, full(wide_o, source, end), first)
+
+        @pl.when(is_hub)
+        def _():
+            for j in range(held):
+                own_block(j)
+                pass_block(j)
+            settle(ma, True, True)
+            for j in range(held):
                 other_block(j)
-                finish(j, j + 1, full(last, j))
-
-        @pl.when(jnp.logical_not(direct))
-        def _():
-            for j in range(splits):
-                if j > 0:
-                    own_block(j)
-                    relay(last, j, p_send.at[2] if j < end else d_send, p_last.at[j])
-                add_to(j, half(last, j, j + 1, pol))
-                if 0 < j < end:
-                    other_block(j - 1)
-                    finish(j - 1, j, half(last, j - 1, j, 1 - pol))
-            other_block(end - 1)
+                add_to(acc, j, full(wide, last, j))
+            for k in range(n_ma - 2):
+                take(k)
+                if k:
+                    settle(order[k - 1], False, True)
+            if n_ma > 2:
+                settle(order[n_ma - 3], False, True)
+
+        @pl.when(hub_lead)
+        def _():
+            with mark("y0"):
+                await_all(part(last, 0, held), y_last.at[0])
+            pass_block(held, 0, end)
+            own_block(held)
+            pass_block(held)
+            for j in range(held):
+                finish(acc, inv_n, j)
+            finish(acc, inv_n, held, full(wide, last, held))
+            with mark("y1"):
+                await_all(part(last, 0, end), y_last.at[1])
+            add_to(acc, end, half(wide, last, end, 0))
+            add_to(acc_o, 0, half(wide_o, last, end, 0))
+            own_block(end)
+            finish_both(half(wide, last, end, 1), half(wide_o, last, end, 1))
+
+        @pl.when(hub_other)
+        def _():
+            for j in range(held):
+                finish(acc, inv_n, j)
+            with mark("x"):
+                await_all(part(last, 0, held), p_last.at[end])
+            other_block(held)
+            finish(acc, inv_n, held, full(wide, last, held))
+
+        @pl.when(jnp.logical_not(is_hub))
+        def _():
+            before = ma
+            for k in range(n_ma - 2):
+                take(k)
+                settle(before, k == 0)
+                before = order[k]
+            own_block(0)
+            pass_block(0)
+            settle(before)
+            add_to(acc, 0, half(wide, last, 0, pol))
+            for j in range(1, splits):
+                own_block(j)
+                pass_block(j)
+                add_to(acc, j, half(wide, last, j, pol))
+                other_block(j - 1)
+                finish(acc, inv_n, j - 1, half(wide, last, j - 1, 1 - pol))
             other_block(end)
-            finish(end - 1, splits, half(last, end - 1, splits, 1 - pol))
+            finish(acc, inv_n, end, half(wide, last, end, 1 - pol))
     else:
         def pass_on(source):
             @pl.when(source != ma)
@@ -363,7 +434,7 @@
         for g in range(groups):
             add(g, g == 0)
         for j in range(splits):
-            finish(j, j + 1)
+            finish(acc, inv_n, j)
 
     row = jnp.sum(total_ref[...], axis=0, keepdims=True)
     mine[0:1, :] = row
@@ -376,15 +447,34 @@
             device_id=place(lax.rem(my_slot + r, n_all)), device_id_type=MESH).start()
 
     for_peers(report)
+    if few:
+        @pl.when(hub_lead)
+        def _():
+            push(acc_o, incoming, i_send, i_recv, {"pol": 0})
 
     with mark("drain"):
-        await_all(planes.at[pl.ds(0, n_ma - 1)], z_send)
+        await_all(planes.at[pl.ds(0, n_ma - 2 if few else n_ma - 1)], z_send)
         await_all(planes.at[0], p_send.at[0])
         if few:
             if n_ma > 2:
                 await_all(planes.at[pl.ds(0, n_ma - 2)], p_send.at[1])
-            await_all(planes.at[0, pl.ds(0, splits - 1)], p_send.at[2])
-            await_all(planes.at[0, 0], d_send)
+            await_all(planes.at[0], near_send)
+            for where, count in ((hub_other, held), (jnp.logical_not(hub_other), splits)):
+                @pl.when(where)
+                def _():
+                    await_all(planes.at[0, pl.ds(0, count)], p_send.at[2])
+
+            @pl.when(hub_lead)
+            def _():
+                await_all(extra, x_send)
+
+            @pl.when(hub_other)
+            def _():
+                await_all(beam_o, b_send.at[0])
+                await_all(noise_o, b_send.at[1])
+                with mark("incoming"):
+                    await_all(incoming, i_recv)
+                acc[:, end * lanes:] = incoming[...]
         else:
             await_all(planes.at[pl.ds(0, n_ma - 1)], p_send.at[1])
     with mark("heard"):
@@ -404,6 +494,10 @@
     power_ref[...] = jnp.broadcast_to(here, power_ref.shape)
     scale_ref[...] = rs_n[...] * factor
     await_all(slots.at[pl.ds(0, n_all - 1)], q_send)
+    if few:
+        @pl.when(hub_lead)
+        def _():
+            await_all(acc_o, i_send)
     tail.__exit__(None,None,None)
 
 
@@ -460,16 +554,24 @@
         scratch_shapes=[
             pltpu.VMEM((2, block, n_ma, columns), jnp.bfloat16),
             pltpu.VMEM((n_ma, splits, 2, block, LANES), jnp.bfloat16),
+            pltpu.VMEM((2, 2, block, LANES), jnp.bfloat16),
             pltpu.VMEM((groups, splits, 2, rows, LANES), jnp.bfloat16),
             pltpu.VMEM((groups, 2 * modes, 2 * rows), jnp.bfloat16),
+            pltpu.VMEM((groups, 2 * modes, 2 * rows), jnp.bfloat16),
             pltpu.VMEM((2, modes, degrees), jnp.bfloat16),
+            pltpu.VMEM((2, modes, degrees), jnp.bfloat16),
+            pltpu.VMEM((2 * modes, LANES), jnp.float32),
+            pltpu.VMEM((2 * modes, LANES), jnp.float32),
+            pltpu.VMEM((modes, LANES), jnp.float32),
             pltpu.VMEM((modes, LANES), jnp.float32),
             pltpu.VMEM((modes, LANES), jnp.float32),
             pltpu.VMEM((2, LANES), jnp.float32),
             pltpu.VMEM((n_all, 2, LANES), jnp.float32),
             pltpu.VMEM((8, LANES), jnp.float32),
             pltpu.VMEM((1, modes), jnp.float32),
-            dma, dma((n_ma,)), dma((splits,)), dma, dma((3,)), dma((n_ma,)), dma((splits,)),
+            pltpu.VMEM((1, modes), jnp.float32),
+            dma, dma, dma, dma, dma((2,)), dma((2,)), dma, dma,
+            dma((n_ma,)), dma((splits,)), dma((2,)), dma((3,)), dma((n_ma,)), dma((splits,)),
             dma((splits,)), dma, dma, dma,
             pltpu.SemaphoreType.REGULAR((2,)), pltpu.SemaphoreType.REGULAR((2,)), dma,
         ],

time: 35.7 us -> 35.1 us (0.983)
  Pallas kernels: 33.5 us -> 33 us
    pallas_call x1, Pallas kernels: 32.5 us -> 31.9 us  [on_device(): pl.pallas_call(functools.partial(step_kernel, sizes, total), out_shape=(j...]
where the time goes in v4:
time: 35.1 us; the launch traced here: 34.9 us
  Pallas kernels  33 us (94%)
  between operations  1.93 us (5%)
    pallas_call x1, Pallas kernels, on_device(): pl.pallas_call(functools.partial(step_kernel, sizes, total), out_shape=(j...  31.9 us
    pallas_call x1, Pallas kernels, on_device(): pl.pallas_call(rescale_kernel, out_shape=(jax.ShapeDtypeStruct((2, modes,...  1.07 us

profile of v4, /device:TPU:0, one launch (start us, length us, event | category | flops | bytes accessed | tf_op | source)
XLA Modules:
  0.0 34.9 jit_solution(16875033120399320861)
XLA Ops:
  1.9 31.9 %driftscan_step.1 = (f32[1024,512]{1,0:T(8,128)S(1)}, f32[512,128]{1,0:T(8,128)S(1)}, f32[1,128]{1,0:T(1,128)S(1)}) custom-call(bf16[2,128,4,512]{3,2,1,0:T(4,128)(2,1)} %bitcast.6, bf16[2,512,1024]{2,1,0:T(8,128)(2,1)} %bitcast.5, s32[1]{0:T(128)S(6)} %copy.8.m_ref, s32[1]{0:T(128)S(6)} %copy.9.mask_ref, f32[1,512]{1,0:T(1,128)} %noise_hbm.1), custom_call_target="tpu_custom_call" | custom-call | tf_op jit(solution)/shard_map/driftscan_step/pallas_call | solution.py:545
  33.8 1.1 %rescale.1 = (bf16[2,512,512]{2,1,0:T(8,128)(2,1)}, f32[1]{0:T(128)}) custom-call(f32[1024,512]{1,0:T(8,128)S(1)} %get-tuple-element.7.acc, f32[512,128]{1,0:T(8,128)S(1)} %get-tuple-element.8.scale_ref, f32[1,128]{1,0:T(1,128)S(1)} %get-tuple-element.9.power_ref), custom_call_target="tpu_custom_call" | custom-call | tf_op jit(solution)/shard_map/rescale/pallas_call | solution.py:582

commit v5 on v4

--- a/solution.py
+++ b/solution.py
@@ -39,9 +39,9 @@
 
 def step_kernel(
     sizes, total, alm_hbm, beam_hbm, m_ref, mask_ref, noise_hbm, acc, scale_ref, power_ref,
-    staged, planes, extra, recv, wide, wide_o, beam_v, beam_o, acc_o, incoming, inv_n, inv_o, rs_n, mine, slots, total_ref,
+    staged, planes, extra, guest, recv, wide, wide_o, beam_v, beam_o, acc_o, incoming, inv_n, inv_o, rs_n, mine, slots, total_ref,
     noise_ref, noise_o,
-    z_send, near_send, x_send, x_recv, b_send, b_recv, i_send, i_recv, z_far, z_last, y_last, p_send, p_far, p_last, in_sem, beam_sem, q_send, q_recv, edge, meet, small_sem,
+    z_send, near_send, g_send, g_recv, x_send, x_recv, b_send, b_recv, i_send, i_recv, z_far, z_last, y_last, p_send, p_far, p_last, in_sem, beam_sem, q_send, q_recv, edge, meet, small_sem,
 ):
     n_ma, n_freq, n_pol = sizes
     n_all = n_ma * n_freq * n_pol
@@ -78,6 +78,7 @@
     inward, outward = jnp.where(below, ma + 1, ma - 1), jnp.where(below, ma - 1, ma + 1)
     is_hub = jnp.logical_or(ma == low - 1, ma == low)
     has_outward = jnp.logical_and(ma > 0, ma < n_ma - 1)
+    odd = lax.rem(freq, 2) == 1
     hub_lead, hub_other = jnp.logical_and(is_hub, pol == 1), jnp.logical_and(is_hub, pol == 0)
 
     def tell_line(there, sem):
@@ -172,10 +173,24 @@
             if now:
                 @pl.when(ma == i)
                 def _():
+                    def go(t, j):
+                        send(t, j, z_last.at[j] if i == across(n_ma, t) else z_far.at[i],
+                             near_send if t == near else z_send)
+
                     for t, j in now:
-                        if (t, j) not in late:
-                            send(t, j, z_last.at[j] if i == across(n_ma, t) else z_far.at[i],
-                                 near_send if t == near else z_send)
+                        if hub and (t, j) == (near, 1):
+                            detour = jnp.logical_and(odd, pol == 1)
+
+                            @pl.when(detour)
+                            def _():
+                                push(planes.at[t, j, 0], guest, near_send, g_recv, {"freq": freq - 1})
+                                push(planes.at[t, j, 1], part(ma, pol, j).at[1], near_send, z_last.at[j], {"ma": t})
+
+                            @pl.when(jnp.logical_not(detour))
+                            def _():
+                                go(t, j)
+                        elif (t, j) not in late:
+                            go(t, j)
                     if late:
                         @pl.when(pol == 0)
                         def _():
@@ -187,6 +202,14 @@
                             for t, j in late:
                                 push(extra.at[j - held], part(ma, 0, j), x_send, y_last.at[j - held], {"ma": t})
                                 send(t, j, z_last.at[j], near_send)
+
+    has_guest = jnp.logical_and(hub_lead, jnp.logical_and(jnp.logical_not(odd), freq < n_freq - 1))
+
+    def forward_guest():
+        @pl.when(has_guest)
+        def _():
+            await_all(guest, g_recv)
+            push(guest, part(ma, pol, 1).at[0], g_send, z_last.at[1], {"ma": inward, "freq": freq + 1})
 
     if few:
         send_phase(0)
@@ -220,6 +243,7 @@
         tell_line(outward, edge.at[1])
 
     if few:
+        forward_guest()
         send_phase(3)
     else:
         for j in range(splits):
@@ -468,6 +492,10 @@
             def _():
                 await_all(extra, x_send)
 
+            @pl.when(has_guest)
+            def _():
+                await_all(guest, g_send)
+
             @pl.when(hub_other)
             def _():
                 await_all(beam_o, b_send.at[0])
@@ -555,6 +583,7 @@
             pltpu.VMEM((2, block, n_ma, columns), jnp.bfloat16),
             pltpu.VMEM((n_ma, splits, 2, block, LANES), jnp.bfloat16),
             pltpu.VMEM((2, 2, block, LANES), jnp.bfloat16),
+            pltpu.VMEM((block, LANES), jnp.bfloat16),
             pltpu.VMEM((groups, splits, 2, rows, LANES), jnp.bfloat16),
             pltpu.VMEM((groups, 2 * modes, 2 * rows), jnp.bfloat16),
             pltpu.VMEM((groups, 2 * modes, 2 * rows), jnp.bfloat16),
@@ -570,7 +599,7 @@
             pltpu.VMEM((8, LANES), jnp.float32),
             pltpu.VMEM((1, modes), jnp.float32),
             pltpu.VMEM((1, modes), jnp.float32),
-            dma, dma, dma, dma, dma((2,)), dma((2,)), dma, dma,
+            dma, dma, dma, dma, dma, dma, dma((2,)), dma((2,)), dma, dma,
             dma((n_ma,)), dma((splits,)), dma((2,)), dma((3,)), dma((n_ma,)), dma((splits,)),
             dma((splits,)), dma, dma, dma,
             pltpu.SemaphoreType.REGULAR((2,)), pltpu.SemaphoreType.REGULAR((2,)), dma,

time: 35.1 us -> 34.8 us (level)
  no operation moved by 1% of the time
where the time goes in v5:
time: 34.8 us; the launch traced here: 34.6 us
  Pallas kernels  32.7 us (94%)
  between operations  1.93 us (6%)
    pallas_call x1, Pallas kernels, on_device(): pl.pallas_call(functools.partial(step_kernel, sizes, total), out_shape=(j...  31.6 us
    pallas_call x1, Pallas kernels, on_device(): pl.pallas_call(rescale_kernel, out_shape=(jax.ShapeDtypeStruct((2, modes,...  1.07 us

profile of v5, /device:TPU:0, one launch (start us, length us, event | category | flops | bytes accessed | tf_op | source)
XLA Modules:
  0.0 34.6 jit_solution(9407747813457082061)
XLA Ops:
  1.9 31.6 %driftscan_step.1 = (f32[1024,512]{1,0:T(8,128)S(1)}, f32[512,128]{1,0:T(8,128)S(1)}, f32[1,128]{1,0:T(1,128)S(1)}) custom-call(bf16[2,128,4,512]{3,2,1,0:T(4,128)(2,1)} %bitcast.6, bf16[2,512,1024]{2,1,0:T(8,128)(2,1)} %bitcast.5, s32[1]{0:T(128)S(6)} %copy.8.m_ref, s32[1]{0:T(128)S(6)} %copy.9.mask_ref, f32[1,512]{1,0:T(1,128)} %noise_hbm.1), custom_call_target="tpu_custom_call" | custom-call | tf_op jit(solution)/shard_map/driftscan_step/pallas_call | solution.py:573
  33.5 1.1 %rescale.1 = (bf16[2,512,512]{2,1,0:T(8,128)(2,1)}, f32[1]{0:T(128)}) custom-call(f32[1024,512]{1,0:T(8,128)S(1)} %get-tuple-element.7.acc, f32[512,128]{1,0:T(8,128)S(1)} %get-tuple-element.8.scale_ref, f32[1,128]{1,0:T(1,128)S(1)} %get-tuple-element.9.power_ref), custom_call_target="tpu_custom_call" | custom-call | tf_op jit(solution)/shard_map/rescale/pallas_call | solution.py:611

commit v6 on v5

--- a/solution.py
+++ b/solution.py
@@ -41,7 +41,7 @@
     sizes, total, alm_hbm, beam_hbm, m_ref, mask_ref, noise_hbm, acc, scale_ref, power_ref,
     staged, planes, extra, guest, recv, wide, wide_o, beam_v, beam_o, acc_o, incoming, inv_n, inv_o, rs_n, mine, slots, total_ref,
     noise_ref, noise_o,
-    z_send, near_send, g_send, g_recv, x_send, x_recv, b_send, b_recv, i_send, i_recv, z_far, z_last, y_last, p_send, p_far, p_last, in_sem, beam_sem, q_send, q_recv, edge, meet, small_sem,
+    z_send, near_send, g_send, g_recv, c_send, c_recv, z_far, z_last, p_send, p_far, p_last, in_sem, beam_sem, q_send, q_recv, edge, meet, small_sem,
 ):
     n_ma, n_freq, n_pol = sizes
     n_all = n_ma * n_freq * n_pol
@@ -194,13 +194,13 @@
                     if late:
                         @pl.when(pol == 0)
                         def _():
-                            push(planes.at[near, pl.ds(held, 2)], extra, near_send, x_recv, {"pol": 1})
+                            push(planes.at[near, pl.ds(held, 2)], extra, near_send, c_recv.at[2], {"pol": 1})
 
                         @pl.when(pol == 1)
                         def _():
-                            await_all(extra, x_recv)
+                            await_all(extra, c_recv.at[2])
                             for t, j in late:
-                                push(extra.at[j - held], part(ma, 0, j), x_send, y_last.at[j - held], {"ma": t})
+                                push(extra.at[j - held], part(ma, 0, j), c_send.at[0], p_last.at[j], {"ma": t})
                                 send(t, j, z_last.at[j], near_send)
 
     has_guest = jnp.logical_and(hub_lead, jnp.logical_and(jnp.logical_not(odd), freq < n_freq - 1))
@@ -257,8 +257,8 @@
     if few:
         @pl.when(hub_other)
         def _():
-            push(beam_hbm, beam_o, b_send.at[0], b_recv.at[0], {"pol": 1})
-            push(noise_hbm, noise_o, b_send.at[1], b_recv.at[1], {"pol": 1})
+            push(beam_hbm, beam_o, c_send.at[0], c_recv.at[0], {"pol": 1})
+            push(noise_hbm, noise_o, c_send.at[1], c_recv.at[1], {"pol": 1})
 
     noise_copy.wait()
     spread = jnp.transpose(jnp.broadcast_to(noise_ref[...], (LANES, modes)))
@@ -291,9 +291,9 @@
     if few:
         @pl.when(hub_lead)
         def _():
-            await_all(noise_o, b_recv.at[1])
+            await_all(noise_o, c_recv.at[1])
             inv_o[...] = 1.0 / jnp.transpose(jnp.broadcast_to(noise_o[...], (LANES, modes)))
-            await_all(beam_o, b_recv.at[0])
+            await_all(beam_o, c_recv.at[0])
             loop(0, modes // strip, functools.partial(widen, beam_o, wide_o))
 
     tile = min(modes, 256)
@@ -367,13 +367,13 @@
 
         def pass_block(j, core=None, slot=None):
             at = part(last, pol if core is None else core, j)
-            push(at, at, p_send.at[2], p_last.at[j if slot is None else slot], {"pol": 1 - pol})
+            push(at, at, p_send.at[1], p_last.at[j if slot is None else slot], {"pol": 1 - pol})
 
         def take(k):
             with mark(f"wait{k}"):
                 await_all(whole(order[k], pol), z_far.at[order[k]])
             for j in range(splits):
-                relay(order[k], j, p_send.at[1], p_far.at[order[k]])
+                relay(order[k], j, p_send.at[0], p_far.at[order[k]])
 
         def settle(source, first=False, shared=False):
             with mark("relay"):
@@ -404,7 +404,7 @@
         @pl.when(hub_lead)
         def _():
             with mark("y0"):
-                await_all(part(last, 0, held), y_last.at[0])
+                await_all(part(last, 0, held), p_last.at[held])
             pass_block(held, 0, end)
             own_block(held)
             pass_block(held)
@@ -412,7 +412,7 @@
                 finish(acc, inv_n, j)
             finish(acc, inv_n, held, full(wide, last, held))
             with mark("y1"):
-                await_all(part(last, 0, end), y_last.at[1])
+                await_all(part(last, 0, end), p_last.at[end])
             add_to(acc, end, half(wide, last, end, 0))
             add_to(acc_o, 0, half(wide_o, last, end, 0))
             own_block(end)
@@ -424,8 +424,9 @@
                 finish(acc, inv_n, j)
             with mark("x"):
                 await_all(part(last, 0, held), p_last.at[end])
+            add_to(acc, held, half(wide, last, held, 0))
             other_block(held)
-            finish(acc, inv_n, held, full(wide, last, held))
+            finish(acc, inv_n, held, half(wide, last, held, 1))
 
         @pl.when(jnp.logical_not(is_hub))
         def _():
@@ -452,7 +453,7 @@
             def _():
                 await_all(whole(source, pol), z_far.at[source])
                 for j in range(splits):
-                    relay(source, j, p_send.at[1], p_far.at[source])
+                    relay(source, j, p_send.at[0], p_far.at[source])
         loop(0, n_ma, pass_on)
         loop(0, n_ma, relayed)
         for g in range(groups):
@@ -474,23 +475,21 @@
     if few:
         @pl.when(hub_lead)
         def _():
-            push(acc_o, incoming, i_send, i_recv, {"pol": 0})
+            push(acc_o, incoming, c_send.at[1], c_recv.at[0], {"pol": 0})
 
     with mark("drain"):
         await_all(planes.at[pl.ds(0, n_ma - 2 if few else n_ma - 1)], z_send)
-        await_all(planes.at[0], p_send.at[0])
+        await_all(planes.at[pl.ds(0, n_ma - 1)] if few else planes, p_send.at[0])
         if few:
-            if n_ma > 2:
-                await_all(planes.at[pl.ds(0, n_ma - 2)], p_send.at[1])
             await_all(planes.at[0], near_send)
             for where, count in ((hub_other, held), (jnp.logical_not(hub_other), splits)):
                 @pl.when(where)
                 def _():
-                    await_all(planes.at[0, pl.ds(0, count)], p_send.at[2])
+                    await_all(planes.at[0, pl.ds(0, count)], p_send.at[1])
 
             @pl.when(hub_lead)
             def _():
-                await_all(extra, x_send)
+                await_all(extra, c_send.at[0])
 
             @pl.when(has_guest)
             def _():
@@ -498,13 +497,11 @@
 
             @pl.when(hub_other)
             def _():
-                await_all(beam_o, b_send.at[0])
-                await_all(noise_o, b_send.at[1])
+                await_all(beam_o, c_send.at[0])
+                await_all(noise_o, c_send.at[1])
                 with mark("incoming"):
-                    await_all(incoming, i_recv)
+                    await_all(incoming, c_recv.at[0])
                 acc[:, end * lanes:] = incoming[...]
-        else:
-            await_all(planes.at[pl.ds(0, n_ma - 1)], p_send.at[1])
     with mark("heard"):
         await_all(slots.at[pl.ds(0, n_all - 1)], q_recv)
 
@@ -525,7 +522,7 @@
     if few:
         @pl.when(hub_lead)
         def _():
-            await_all(acc_o, i_send)
+            await_all(acc_o, c_send.at[1])
     tail.__exit__(None,None,None)
 
 
@@ -599,8 +596,7 @@
             pltpu.VMEM((8, LANES), jnp.float32),
             pltpu.VMEM((1, modes), jnp.float32),
             pltpu.VMEM((1, modes), jnp.float32),
-            dma, dma, dma, dma, dma, dma, dma((2,)), dma((2,)), dma, dma,
-            dma((n_ma,)), dma((splits,)), dma((2,)), dma((3,)), dma((n_ma,)), dma((splits,)),
+            dma, dma, dma, dma, dma((2,)), dma((3,)), dma((n_ma,)), dma((splits,)), dma((2,)), dma((n_ma,)), dma((splits,)),
             dma((splits,)), dma, dma, dma,
             pltpu.SemaphoreType.REGULAR((2,)), pltpu.SemaphoreType.REGULAR((2,)), dma,
         ],

time: 34.8 us -> 34.7 us (level)
  no operation moved by 1% of the time
where the time goes in v6:
time: 34.7 us; the launch traced here: 34.5 us
  Pallas kernels  32.6 us (94%)
  between operations  1.93 us (6%)
    pallas_call x1, Pallas kernels, on_device(): pl.pallas_call(functools.partial(step_kernel, sizes, total), out_shape=(j...  31.5 us
    pallas_call x1, Pallas kernels, on_device(): pl.pallas_call(rescale_kernel, out_shape=(jax.ShapeDtypeStruct((2, modes,...  1.07 us

profile of v6, /device:TPU:0, one launch (start us, length us, event | category | flops | bytes accessed | tf_op | source)
XLA Modules:
  0.0 34.5 jit_solution(1454712572969316185)
XLA Ops:
  1.9 31.5 %driftscan_step.1 = (f32[1024,512]{1,0:T(8,128)S(1)}, f32[512,128]{1,0:T(8,128)S(1)}, f32[1,128]{1,0:T(1,128)S(1)}) custom-call(bf16[2,128,4,512]{3,2,1,0:T(4,128)(2,1)} %bitcast.6, bf16[2,512,1024]{2,1,0:T(8,128)(2,1)} %bitcast.5, s32[1]{0:T(128)S(6)} %copy.8.m_ref, s32[1]{0:T(128)S(6)} %copy.9.mask_ref, f32[1,512]{1,0:T(1,128)} %noise_hbm.1), custom_call_target="tpu_custom_call" | custom-call | tf_op jit(solution)/shard_map/driftscan_step/pallas_call | solution.py:570
  33.5 1.1 %rescale.1 = (bf16[2,512,512]{2,1,0:T(8,128)(2,1)}, f32[1]{0:T(128)}) custom-call(f32[1024,512]{1,0:T(8,128)S(1)} %get-tuple-element.7.acc, f32[512,128]{1,0:T(8,128)S(1)} %get-tuple-element.8.scale_ref, f32[1,128]{1,0:T(1,128)S(1)} %get-tuple-element.9.power_ref), custom_call_target="tpu_custom_call" | custom-call | tf_op jit(solution)/shard_map/rescale/pallas_call | solution.py:607
